TPU v7x, 256 devices: a whole 4x4x8 slice. The times are simulated.
256 devices in a mesh: facet: 64 (over z, y, core), col: 4 (over x).
Axes of the slice: x: 4, y: 4, z: 8, core: 2. Of those that a mesh axis runs over, the one named last changes fastest.
Arguments:
- strip: bfloat16 [2, 64, 262144], P(None, None, 'facet'), may hold values from -6 to 6
- screen_first: bfloat16 [2, 512, 512], replicated, may hold values from -1 to 1
- screen_second: bfloat16 [2, 512, 512], replicated, may hold values from -1 to 1
- owners: int32 [4, 4096, 3], P('col', 'facet'), may hold values from 0 to 127, all different within a row; in each aligned block of 64 rows (0 to 63, 64 to 127, ..., all dimensions but the last counted through in order) at most 2 rows name the same one
- live: int32 [4, 4096, 3], P('col', 'facet'), may hold values 0 or 1
- place: int32 [4, 4096, 3], P('col', 'facet'), may hold values from 0 to 63
Outputs:
- facet_image: float32 [2, 64, 262144], P(None, None, ('facet', 'col'))
Inputs may be any that keep to these rules, and one draw needn't show every extreme that they name: `owners`: each row names three different subgrids; among the rows of one device no subgrid is named more than 2 times, a bound that some block reaches. `place`: tile p lies at tile row p // 8 and tile column p % 8.
All inputs are finite; a program needn't handle non-finite values. No bound on the sum of `live` on one device may be relied on, other than what follows from the above.
Results may differ from a plain program's by a relative error of at most 0.013.
Values may be sent and summed in bfloat16 or wider, within the bound.
No kernel may reach another device: no remote copies, remote signals or barrier semaphores. Data moves between devices by JAX's collectives and lax.ppermute only.
A program may use at most 64 MiB of HBM per device.

v0:
```python
import math

import jax
import jax.numpy as jnp
from jax import lax
from jax.sharding import PartitionSpec as P

SUB_DEV = 2


def exchange_in_groups(x, axis, split_dim, concat_dim, work, item_dim, out_dim):
    items = jax.tree.leaves(x)[0].shape[item_dim]
    count = 2 if items % 2 == 0 else 1
    gathered = []
    for k in range(count):
        group = jax.tree.map(
            lambda a: lax.slice_in_dim(
                a, k * (items // count), (k + 1) * (items // count), axis=item_dim
            ),
            x,
        )
        gathered.append(
            work(
                lax.all_to_all(
                    group, axis, split_axis=split_dim, concat_axis=concat_dim, tiled=True
                )
            )
        )
    return jax.tree.map(lambda *parts: jnp.concatenate(parts, axis=out_dim), *gathered)


def split_up(x, dim, length):
    dims = x.shape
    pieces = x.reshape(*dims[:dim], length, dims[dim] // length, *dims[dim + 1 :])
    return jnp.moveaxis(pieces, dim, 0)


def summed_on_arrival(x, axis, dim):
    length = lax.axis_size(axis)
    pieces = lax.all_to_all(split_up(x, dim, length), axis, 0, 0, tiled=True)
    return jnp.sum(pieces.astype(jnp.float32), axis=0)


def dft_table(length, direction):
    index = jnp.arange(length, dtype=jnp.int32)
    phase = index[:, None] * index[None, :] % length
    angle = phase.astype(jnp.float32) * (2.0 * math.pi / length)
    scale = 1.0 / math.sqrt(length)
    return (jnp.cos(angle) * scale, direction * jnp.sin(angle) * scale)


def left_apply(table, field):
    real_table, imag_table = table
    real_part, imag_part = field
    real = jnp.dot(real_table, real_part, preferred_element_type=jnp.float32) - jnp.dot(
        imag_table, imag_part, preferred_element_type=jnp.float32
    )
    imag = jnp.dot(real_table, imag_part, preferred_element_type=jnp.float32) + jnp.dot(
        imag_table, real_part, preferred_element_type=jnp.float32
    )
    return (real, imag)


def right_apply(field, table):
    real_table, imag_table = table
    real_part, imag_part = field
    real = jnp.dot(real_part, real_table, preferred_element_type=jnp.float32) - jnp.dot(
        imag_part, imag_table, preferred_element_type=jnp.float32
    )
    imag = jnp.dot(real_part, imag_table, preferred_element_type=jnp.float32) + jnp.dot(
        imag_part, real_table, preferred_element_type=jnp.float32
    )
    return (real, imag)


def screen_apply(field, screen):
    real_part, imag_part = field
    screen_real = screen[0].astype(jnp.float32)
    screen_imag = screen[1].astype(jnp.float32)
    real = real_part * screen_real - imag_part * screen_imag
    imag = real_part * screen_imag + imag_part * screen_real
    return (real.astype(jnp.bfloat16), imag.astype(jnp.bfloat16))


def process_tiles(tiles, screen_first, screen_second, forward, inverse):
    tile_count, width = tiles.shape
    side_tiles = math.isqrt(tile_count)
    win_size = math.isqrt(width // 2)
    sub_size = side_tiles * win_size
    field = (
        tiles.reshape(side_tiles, side_tiles, 2, win_size, win_size)
        .transpose(2, 0, 3, 1, 4)
        .reshape(2, sub_size, sub_size)
    )
    rows = left_apply(forward, (field[0], field[1]))
    rows = (rows[0].astype(jnp.bfloat16), rows[1].astype(jnp.bfloat16))
    spectrum = screen_apply(right_apply(rows, forward), screen_first)
    back = left_apply(inverse, spectrum)
    back = (back[0].astype(jnp.bfloat16), back[1].astype(jnp.bfloat16))
    image = screen_apply(right_apply(back, inverse), screen_second)
    stacked = jnp.stack([image[0], image[1]])
    return (
        stacked.reshape(2, side_tiles, win_size, side_tiles, win_size)
        .transpose(1, 3, 0, 2, 4)
        .reshape(tile_count, width)
    )


def shards(strip, screen_first, screen_second, owners, live, place):
    win_size = strip.shape[1]
    sub_size = screen_first.shape[-1]
    side_tiles = sub_size // win_size
    tile_count = side_tiles * side_tiles
    width = 2 * win_size * win_size
    peer_count = lax.axis_size("facet")
    win_local = strip.shape[2] // win_size
    sub_local = SUB_DEV
    subgrid_count = sub_local * peer_count
    capacity = max(2, (7 * win_local + 2 * subgrid_count - 1) // (2 * subgrid_count))
    total_slots = subgrid_count * capacity
    small_real, small_imag = dft_table(win_size, -1.0)
    small = (small_real.astype(jnp.bfloat16), small_imag.astype(jnp.bfloat16))
    front = left_apply(small, (strip[0], strip[1]))
    contrib = jnp.stack([front[0], front[1]]).astype(jnp.bfloat16)
    windows = (
        contrib.reshape(2, win_size, win_local, win_size)
        .transpose(2, 0, 1, 3)
        .reshape(win_local, width)
    )
    flat_owner = owners[0].reshape(-1)
    flat_live = live[0].reshape(-1)
    flat_place = place[0].reshape(-1)
    entries = flat_owner.shape[0]
    order_index = jnp.arange(entries, dtype=jnp.int32)
    earlier = (flat_owner[:, None] == flat_owner[None, :]) & (
        order_index[None, :] < order_index[:, None]
    )
    rank = jnp.sum(earlier.astype(jnp.int32), axis=1)
    slot_of = flat_owner * capacity + rank
    slot_index = jnp.arange(total_slots, dtype=jnp.int32)
    hit_rows = ((slot_of[None, :] == slot_index[:, None]) & (flat_live[None, :] == 1)).astype(
        jnp.int32
    )
    hit_cols = ((slot_of[:, None] == slot_index[None, :]) & (flat_live[:, None] == 1)).astype(
        jnp.int32
    )
    codes = jnp.sum(hit_rows * (flat_place[None, :] + 1), axis=1) - 1
    packer = jnp.sum(hit_rows.reshape(total_slots, win_local, 3), axis=2).astype(jnp.bfloat16)
    unpacker = jnp.sum(hit_cols.reshape(win_local, 3, total_slots), axis=1).astype(jnp.bfloat16)
    outgoing = jnp.dot(packer, windows, preferred_element_type=jnp.float32).astype(jnp.bfloat16)
    outgoing = outgoing.reshape(peer_count, sub_local, capacity, width)
    codes = codes.reshape(peer_count, sub_local, capacity)
    big_real, big_imag = dft_table(sub_size, -1.0)
    forward = (big_real.astype(jnp.bfloat16), big_imag.astype(jnp.bfloat16))
    inverse = (big_real.astype(jnp.bfloat16), (-big_imag).astype(jnp.bfloat16))
    tile_index = jnp.arange(tile_count, dtype=jnp.int32)

    def handle(received):
        parcels, labels = received
        item_count = parcels.shape[1]
        sources = parcels.shape[0]
        stacked = parcels.transpose(1, 0, 2, 3).reshape(item_count, sources * capacity, width)
        marks = labels.transpose(1, 0, 2).reshape(item_count, sources * capacity)

        def one_subgrid(pair):
            slabs, tags = pair
            embed_map = (tags[None, :] == tile_index[:, None]).astype(jnp.bfloat16)
            cut_map = (tags[:, None] == tile_index[None, :]).astype(jnp.bfloat16)
            tiles = jnp.dot(embed_map, slabs, preferred_element_type=jnp.float32).astype(
                jnp.bfloat16
            )
            finished = process_tiles(tiles, screen_first, screen_second, forward, inverse)
            return jnp.dot(cut_map, finished, preferred_element_type=jnp.float32).astype(
                jnp.bfloat16
            )

        result = lax.map(one_subgrid, (stacked, marks))
        return result.reshape(item_count, sources, capacity, width).transpose(1, 0, 2, 3)

    def handle_and_return(received):
        return lax.all_to_all(handle(received), "facet", split_axis=0, concat_axis=0, tiled=True)

    returned = exchange_in_groups((outgoing, codes), "facet", 0, 0, handle_and_return, 1, 1)
    summed = jnp.dot(
        unpacker, returned.reshape(total_slots, width), preferred_element_type=jnp.float32
    )
    field = (
        summed.reshape(win_local, 2, win_size, win_size)
        .transpose(1, 2, 0, 3)
        .reshape(2, win_size, win_local * win_size)
    )
    column = summed_on_arrival(field.astype(jnp.bfloat16), "col", 2)
    back_real, back_imag = dft_table(win_size, 1.0)
    highest = lax.Precision.HIGHEST
    real = jnp.dot(back_real, column[0], precision=highest) - jnp.dot(
        back_imag, column[1], precision=highest
    )
    imag = jnp.dot(back_real, column[1], precision=highest) + jnp.dot(
        back_imag, column[0], precision=highest
    )
    return jnp.stack([real, imag])


def solution(mesh):
    placed = (
        P(None, None, "facet"),
        P(),
        P(),
        P("col", "facet", None),
        P("col", "facet", None),
        P("col", "facet", None),
    )
    return jax.shard_map(
        shards,
        mesh=mesh,
        in_specs=placed,
        out_specs=P(None, None, ("facet", "col")),
        check_vma=False,
    )
```

profile of v0, /device:TPU:32, one launch (start us, length us, event | category | flops | bytes accessed | tf_op | source)
XLA Modules:
  0.0 492.2 jit_solution(9788124412131558751)
XLA Ops:
  4.1 11.8 %all-to-all-start = ((s32[64,1,2]{2,1,0:T(1,128)}), s32[64,1,2]{2,1,0:T(1,128)S(1)}, u32[]{:S(2)}, u32[]{:S(2)}) async-start(s32[64,1,2]{2,1,0:T(1,128)} %get-tuple-element.133), calls=%async_computation | async-start | bytes 65536 | tf_op jit(solution)/shard_map/all_to_all | solution.py:24
  32.4 7.6 %reshape.176 = bf16[64,2,2,8192]{3,2,1,0:T(2,128)(2,1)} reshape(bf16[256,8192]{1,0:T(8,128)(2,1)} %convolution_convert_fusion) | data formatting | bytes 8388608 | tf_op jit(solution)/shard_map/reshape | solution.py:151
  40.0 10.3 %all-to-all-start.3 = ((s32[64,1,2]{2,1,0:T(1,128)}), s32[64,1,2]{2,1,0:T(1,128)S(1)}, u32[]{:S(2)}, u32[]{:S(2)}) async-start(s32[64,1,2]{2,1,0:T(1,128)} %get-tuple-element.134), calls=%async_computation.3 | async-start | bytes 65536 | tf_op jit(solution)/shard_map/all_to_all | solution.py:24
  50.3 6.5 %fusion.302 = (bf16[64,1,2,8192]{3,2,1,0:T(2,128)(2,1)}, bf16[64,1,2,8192]{3,2,1,0:T(2,128)(2,1)S(1)}) fusion(bf16[64,2,2,8192]{3,2,1,0:T(2,128)(2,1)} %reshape.176), kind=kLoop, calls=%fused_computation.370 | loop fusion | bytes 8388608 | tf_op jit(solution)/shard_map/slice | solution.py:17
  59.0 65.1 %all_to_all.35 = bf16[64,1,2,8192]{3,2,1,0:T(2,128)(2,1)} all-to-all(bf16[64,1,2,8192]{3,2,1,0:T(2,128)(2,1)S(1)} %get-tuple-element.116), channel_id=1, replica_groups=mesh['facet'=64,'col'=4] {'facet'}, dimensions={0} | all-to-all | bytes 4194304 | tf_op jit(solution)/shard_map/all_to_all | solution.py:24
  124.1 6.3 %all-to-all-start.1 = ((bf16[64,1,2,8192]{3,2,1,0:T(2,128)(2,1)}), bf16[64,1,2,8192]{3,2,1,0:T(2,128)(2,1)S(1)}, u32[]{:S(2)}, u32[]{:S(2)}) async-start(bf16[64,1,2,8192]{3,2,1,0:T(2,128)(2,1)} %get-tuple-element.115), calls=%async_computation.1 | async-start | bytes 4194304 | tf_op jit(solution)/shard_map/all_to_all | solution.py:24
  155.6 5.1 %fusion.44 = f32[512,512]{1,0:T(8,128)} fusion(bf16[512,512]{1,0:T(8,128)(2,1)S(1)} %copy-done.5), kind=kOutput, calls=%fused_computation.101 | convolution fusion | flops 272629760 | bytes 1572864 | tf_op jit(solution)/shard_map/while/body/eval_jaxpr/dot_general | solution.py:58
  165.3 6.0 %fusion.53 = f32[512,512]{1,0:T(8,128)} fusion(bf16[512,512]{1,0:T(8,128)(2,1)S(1)} %fusion.6), kind=kOutput, calls=%fused_computation.110 | convolution fusion | flops 272629760 | bytes 1572864 | tf_op jit(solution)/shard_map/while/body/eval_jaxpr/dot_general | solution.py:70
  171.3 5.7 %fusion.45 = f32[512,512]{1,0:T(8,128)} fusion(bf16[512,512]{1,0:T(8,128)(2,1)S(1)} %fusion.6), kind=kOutput, calls=%fused_computation.102 | convolution fusion | flops 272629760 | bytes 1572864 | tf_op jit(solution)/shard_map/while/body/eval_jaxpr/dot_general | solution.py:67
  189.9 5.5 %fusion.52 = f32[512,512]{1,0:T(8,128)} fusion(bf16[512,512]{1,0:T(8,128)(2,1)S(1)} %squeeze.77), kind=kOutput, calls=%fused_computation.109 | convolution fusion | flops 272629760 | bytes 1572864 | tf_op jit(solution)/shard_map/while/body/eval_jaxpr/dot_general | solution.py:55
  228.6 5.1 %convolution_subtract_fusion.3 = f32[512,512]{1,0:T(8,128)S(1)} fusion(f32[512,512]{1,0:T(8,128)S(1)} %copy-done.8, bf16[512,512]{1,0:T(8,128)(2,1)S(1)} %fusion.7), kind=kOutput, calls=%fused_computation.41 | convolution fusion | flops 272891904 | bytes 2621440 | tf_op jit(solution)/shard_map/while/body/eval_jaxpr/dot_general | solution.py:67
  238.8 5.4 %fusion.18 = (bf16[512,512]{1,0:T(8,128)(2,1)S(1)}, bf16[512,512]{1,0:T(8,128)(2,1)S(1)}, bf16[512,512]{1,0:T(8,128)(2,1)S(1)}, bf16[512,512]{1,0:T(8,128)(2,1)S(1)}) fusion(f32[512,512]{1,0:T(8,128)S(1)} %convolution_add_fusion.7, bf16[2,512,512]{2,1,0:T(8,128)(2,1)S(1)} %copy-done.6, f32[512,512]{1,0:T(8,128)S(1)} %convolution_add_fusion.3, ...), kind=kOutput, calls=%fused_computation.70 | convolution fusion | flops 277610496 | bytes 7864320 | tf_op jit(solution)/shard_map/while/body/eval_jaxpr/dot_general | solution.py:67
  261.6 5.3 %fusion.42 = f32[512,512]{1,0:T(8,128)S(1)} fusion(bf16[512,512]{1,0:T(8,128)(2,1)S(1)} %fusion.8), kind=kOutput, calls=%fused_computation.99 | convolution fusion | flops 272629760 | bytes 1572864 | tf_op jit(solution)/shard_map/while/body/eval_jaxpr/dot_general | solution.py:67
  303.3 5.1 %convolution_subtract_fusion.1 = f32[512,512]{1,0:T(8,128)S(1)} fusion(f32[512,512]{1,0:T(8,128)S(1)} %fusion.42, bf16[512,512]{1,0:T(8,128)(2,1)S(1)} %fusion.9), kind=kOutput, calls=%fused_computation.37 | convolution fusion | flops 273154048 | bytes 2621440 | tf_op jit(solution)/shard_map/while/body/eval_jaxpr/dot_general | solution.py:67
  308.4 5.3 %convolution_subtract_fusion.5 = f32[512,512]{1,0:T(8,128)S(1)} fusion(f32[512,512]{1,0:T(8,128)S(1)} %fusion.48, bf16[512,512]{1,0:T(8,128)(2,1)S(1)} %fusion.5), kind=kOutput, calls=%fused_computation.45 | convolution fusion | flops 273154048 | bytes 2621440 | tf_op jit(solution)/shard_map/while/body/eval_jaxpr/dot_general | solution.py:67
  313.7 5.9 %fusion.24 = (bf16[512,512]{1,0:T(8,128)(2,1)}, bf16[512,512]{1,0:T(8,128)(2,1)}, bf16[512,512]{1,0:T(8,128)(2,1)S(1)}, bf16[512,512]{1,0:T(8,128)(2,1)S(1)}) fusion(f32[512,512]{1,0:T(8,128)S(1)} %convolution_subtract_fusion.5, bf16[2,512,512]{2,1,0:T(8,128)(2,1)S(1)} %copy-done.7, f32[512,512]{1,0:T(8,128)S(1)} %convolution_add_fusion.1, ...), kind=kOutput, calls=%fused_computation.76 | convolution fusion | flops 277610496 | bytes 7864320 | tf_op jit(solution)/shard_map/while/body/eval_jaxpr/dot_general | solution.py:70
  326.7 6.8 %all-to-all-start.5 = ((bf16[64,1,2,8192]{3,2,1,0:T(2,128)(2,1)}), bf16[64,1,2,8192]{3,2,1,0:T(2,128)(2,1)}, u32[]{:S(2)}, u32[]{:S(2)}) async-start(bf16[64,1,2,8192]{3,2,1,0:T(2,128)(2,1)} %bitcast.19), calls=%async_computation.5 | async-start | bytes 4194304 | tf_op jit(solution)/shard_map/all_to_all | solution.py:181
  340.9 42.9 %all-to-all-done.5 = bf16[64,1,2,8192]{3,2,1,0:T(2,128)(2,1)} async-done(((bf16[64,1,2,8192]{3,2,1,0:T(2,128)(2,1)}), bf16[64,1,2,8192]{3,2,1,0:T(2,128)(2,1)}, u32[]{:S(2)}, u32[]{:S(2)}) %all-to-all-start.5) | async-done | bytes 2097184 | tf_op jit(solution)/shard_map/all_to_all | solution.py:181
  383.8 6.5 %all-to-all-start.2 = ((bf16[64,1,2,8192]{3,2,1,0:T(2,128)(2,1)}), bf16[64,1,2,8192]{3,2,1,0:T(2,128)(2,1)S(1)}, u32[]{:S(2)}, u32[]{:S(2)}) async-start(bf16[64,1,2,8192]{3,2,1,0:T(2,128)(2,1)} %bitcast.16), calls=%async_computation.2 | async-start | bytes 4194304 | tf_op jit(solution)/shard_map/all_to_all | solution.py:181
  390.5 50.3 %all-to-all-done.2 = bf16[64,1,2,8192]{3,2,1,0:T(2,128)(2,1)S(1)} async-done(((bf16[64,1,2,8192]{3,2,1,0:T(2,128)(2,1)}), bf16[64,1,2,8192]{3,2,1,0:T(2,128)(2,1)S(1)}, u32[]{:S(2)}, u32[]{:S(2)}) %all-to-all-start.2) | async-done | bytes 2097184 | tf_op jit(solution)/shard_map/all_to_all | solution.py:181
  440.7 9.1 %pad_maximum_fusion = bf16[64,2,2,8192]{3,2,1,0:T(2,128)(2,1)} fusion(bf16[64,1,2,8192]{3,2,1,0:T(2,128)(2,1)} %all-to-all-done.5, bf16[64,1,2,8192]{3,2,1,0:T(2,128)(2,1)S(1)} %all-to-all-done.2), kind=kLoop, calls=%fused_computation.9 | loop fusion | flops 2097152 | bytes 8388608 | tf_op jit(solution)/shard_map/concatenate | solution.py:29
  449.9 7.2 %reshape.181 = bf16[256,8192]{1,0:T(8,128)(2,1)} reshape(bf16[64,2,2,8192]{3,2,1,0:T(2,128)(2,1)} %pad_maximum_fusion) | data formatting | bytes 8388608 | tf_op jit(solution)/shard_map/reshape | solution.py:185
  457.1 6.4 %copy.62 = bf16[8192,256]{1,0:T(8,128)(2,1)} copy(bf16[8192,256]{0,1:T(8,128)(2,1)} %bitcast.132) | data formatting | bytes 8388608 | tf_op jit(solution)/shard_map/dot_general | solution.py:184
  469.4 19.3 %all_to_all.36 = bf16[4,2,64,1024]{3,2,1,0:T(8,128)(2,1)S(1)} all-to-all(bf16[4,2,64,1024]{3,2,1,0:T(8,128)(2,1)S(1)} %bitcast.135), channel_id=1, replica_groups=mesh['facet'=64,'col'=4] {'col'}, dimensions={0} | all-to-all | bytes 2097152 | tf_op jit(solution)/shard_map/all_to_all | solution.py:40
  (124 shorter events, 180.7 us)
Async XLA Ops:
  0.0 17.3 %copy-start = (bf16[2,64,4096]{2,1,0:T(8,128)(2,1)S(1)}, bf16[2,64,4096]{2,1,0:T(8,128)(2,1)}, u32[]{:S(2)}) copy-start(bf16[2,64,4096]{2,1,0:T(8,128)(2,1)} %param.6) | copy-start | bytes 3145732
  4.1 35.9 %all-to-all-start = ((s32[64,1,2]{2,1,0:T(1,128)}), s32[64,1,2]{2,1,0:T(1,128)S(1)}, u32[]{:S(2)}, u32[]{:S(2)}) async-start(s32[64,1,2]{2,1,0:T(1,128)} %get-tuple-element.133), calls=%async_computation | async-start | bytes 65536 | tf_op jit(solution)/shard_map/all_to_all | solution.py:24
  24.0 2.8 copy-start.1
  40.0 19.0 %all-to-all-start.3 = ((s32[64,1,2]{2,1,0:T(1,128)}), s32[64,1,2]{2,1,0:T(1,128)S(1)}, u32[]{:S(2)}, u32[]{:S(2)}) async-start(s32[64,1,2]{2,1,0:T(1,128)} %get-tuple-element.134), calls=%async_computation.3 | async-start | bytes 65536 | tf_op jit(solution)/shard_map/all_to_all | solution.py:24
  124.1 56.7 %all-to-all-start.1 = ((bf16[64,1,2,8192]{3,2,1,0:T(2,128)(2,1)}), bf16[64,1,2,8192]{3,2,1,0:T(2,128)(2,1)S(1)}, u32[]{:S(2)}, u32[]{:S(2)}) async-start(bf16[64,1,2,8192]{3,2,1,0:T(2,128)(2,1)} %get-tuple-element.115), calls=%async_computation.1 | async-start | bytes 4194304 | tf_op jit(solution)/shard_map/all_to_all | solution.py:24
  150.6 5.1 %copy-start.5 = (bf16[512,512]{1,0:T(8,128)(2,1)S(1)}, bf16[512,512]{1,0:T(8,128)(2,1)}, u32[]{:S(2)}) copy-start(bf16[512,512]{1,0:T(8,128)(2,1)} %squeeze.81) | copy-start | bytes 1572868
  196.1 4.0 copy-start.11
  214.3 4.6 copy-start.2
  214.3 4.5 copy-start.10
  218.9 4.7 copy-start.9
  223.6 5.1 %copy-start.8 = (f32[512,512]{1,0:T(8,128)S(1)}, f32[512,512]{1,0:T(8,128)}, u32[]{:S(2)}) copy-start(f32[512,512]{1,0:T(8,128)} %fusion.45) | copy-start | bytes 3145732
  233.7 5.1 %copy-start.6 = (bf16[2,512,512]{2,1,0:T(8,128)(2,1)S(1)}, bf16[2,512,512]{2,1,0:T(8,128)(2,1)}, u32[]{:S(2)}) copy-start(bf16[2,512,512]{2,1,0:T(8,128)(2,1)} %param.7) | copy-start | bytes 3145732
  308.4 5.3 %copy-start.7 = (bf16[2,512,512]{2,1,0:T(8,128)(2,1)S(1)}, bf16[2,512,512]{2,1,0:T(8,128)(2,1)}, u32[]{:S(2)}) copy-start(bf16[2,512,512]{2,1,0:T(8,128)(2,1)} %param.8) | copy-start | bytes 3145732
  326.7 6.8 %copy-start.4 = (bf16[512,512]{1,0:T(8,128)(2,1)S(1)}, bf16[512,512]{1,0:T(8,128)(2,1)}, u32[]{:S(2)}) copy-start(bf16[512,512]{1,0:T(8,128)(2,1)} %get-tuple-element.118) | copy-start | bytes 1572868
  326.7 57.1 %all-to-all-start.5 = ((bf16[64,1,2,8192]{3,2,1,0:T(2,128)(2,1)}), bf16[64,1,2,8192]{3,2,1,0:T(2,128)(2,1)}, u32[]{:S(2)}, u32[]{:S(2)}) async-start(bf16[64,1,2,8192]{3,2,1,0:T(2,128)(2,1)} %bitcast.19), calls=%async_computation.5 | async-start | bytes 4194304 | tf_op jit(solution)/shard_map/all_to_all | solution.py:181
  333.5 1.0 copy-start.3
  383.8 56.9 %all-to-all-start.2 = ((bf16[64,1,2,8192]{3,2,1,0:T(2,128)(2,1)}), bf16[64,1,2,8192]{3,2,1,0:T(2,128)(2,1)S(1)}, u32[]{:S(2)}, u32[]{:S(2)}) async-start(bf16[64,1,2,8192]{3,2,1,0:T(2,128)(2,1)} %bitcast.16), calls=%async_computation.2 | async-start | bytes 4194304 | tf_op jit(solution)/shard_map/all_to_all | solution.py:181
where the time goes:
time: 502 us; the launch traced here: 492 us
  matrix products  175 us (35%)
  waiting for transfers between devices  99.1 us (20%)
  blocking collectives  84.4 us (17%)
  local copies, waits for them, and re-layouts  76.4 us (15%)
  starting transfers between devices  41.7 us (8%)
  other arithmetic  14.8 us (3%)
    all_to_all x2, waiting for transfers between devices, handle_and_return(): lax.all_to_all(handle(received), 'facet', split_axis=0, concat_axis=0, ti...  93.2 us
    all_to_all x1, blocking collectives, exchange_in_groups(): lax.all_to_all(group, axis, split_axis=split_dim, concat_axis=concat_dim,...  65.1 us
    all_to_all x3, starting transfers between devices, exchange_in_groups(): lax.all_to_all(group, axis, split_axis=split_dim, concat_axis=concat_dim,...  28.4 us
    dot_general x4, matrix products, right_apply(): jnp.dot(imag_part, real_table, preferred_element_type=jnp.float32)  21 us
    dot_general x4, matrix products, right_apply(): jnp.dot(imag_part, imag_table, preferred_element_type=jnp.float32)  20.9 us
    dot_general x4, matrix products, right_apply(): jnp.dot(real_part, real_table, preferred_element_type=jnp.float32)  20.8 us
    dot_general x4, matrix products, right_apply(): jnp.dot(real_part, imag_table, preferred_element_type=jnp.float32)  20.6 us
    dot_general x5, matrix products, left_apply(): jnp.dot(imag_table, real_part, preferred_element_type=jnp.float32)  19.5 us
  transfers between devices with their start and end apart: 5, of which 4 were waited for; matrix products, arithmetic and copies ran while one was open for 17% of the time, Pallas kernels for 0%

commit v1 on v0

v1 whole, which is shorter than its diff:
```python
import functools
import math

import jax
import jax.numpy as jnp
import numpy as np
from jax import lax
from jax.experimental import pallas as pl
from jax.experimental.pallas import tpu as pltpu
from jax.sharding import Mesh, PartitionSpec as P

NZ, NY, NK, NX = 8, 4, 2, 4
WIN = 64
QUARTER = WIN // NX
SUB = 512
SIDE = SUB // WIN
TILES = SIDE * SIDE
CAP = 2
LOCAL = 2
SOURCES = NY * NK
PEERS = SOURCES * NX
SLOTS = NZ * CAP
LANES = 128
BF, F32 = jnp.bfloat16, jnp.float32


def dft(length):
    index = np.arange(length)
    angle = ((index[:, None] * index[None, :]) % length).astype(np.float32) * np.float32(
        2.0 * math.pi / length
    )
    scale = np.float32(1.0 / math.sqrt(length))
    return (
        (np.cos(angle) * scale).astype(np.float32),
        (-np.sin(angle) * scale).astype(np.float32),
    )


def front_table():
    real, imag = dft(WIN)
    both = np.stack(
        [np.concatenate([real, -imag], 1), np.concatenate([imag, real], 1)]
    )
    cut = both.reshape(2, NX, QUARTER, 2 * WIN).transpose(1, 0, 2, 3)
    return cut.reshape(NX, 2 * QUARTER, 2 * WIN).astype(BF)


def left_table():
    real, imag = dft(SUB)
    return np.concatenate([real, imag], 1).astype(BF)


def right_table():
    real, imag = dft(SUB)
    full = np.stack([np.stack([real, imag]), np.stack([-imag, real])])
    full = full.reshape(2, 2, SIDE, WIN, SUB // LANES, LANES)
    return full.transpose(2, 0, 3, 4, 1, 5).reshape(2 * SUB, 2 * SUB).astype(BF)


def last_table():
    real, imag = dft(WIN)
    return np.concatenate([real, -imag], 0).astype(np.float32)


def swap_halves(x):
    return pltpu.roll(x, WIN, x.ndim - 1)


def low_half(shape):
    return lax.broadcasted_iota(jnp.int32, shape, len(shape) - 1) < WIN


def front_kernel(where_ref, table_ref, strip_ref, out_ref):
    table = table_ref[where_ref[0]]
    for j in range(WIN // 2):
        cols = pl.ds(j * LANES, LANES)
        block = jnp.concatenate([strip_ref[0, :, cols], strip_ref[1, :, cols]], 0)
        both = jnp.dot(table, block, preferred_element_type=F32)
        real, imag = both[:QUARTER], both[QUARTER:]
        low = low_half(real.shape)
        out_ref[2 * j] = jnp.where(low, real, swap_halves(imag)).astype(BF)
        out_ref[2 * j + 1] = jnp.where(low, swap_halves(real), imag).astype(BF)


def pack_kernel(extra, rows_ref, *refs):
    blocks, out_ref = list(refs[:9]), refs[-2]
    middle_ref = refs[-1]
    middle_ref[: WIN // 2] = blocks[7][...]
    middle_ref[WIN // 2 :] = blocks[8][...]
    blocks = blocks[:4] + [middle_ref] + blocks[4:7]

    def step(d, carry):
        for j in range(NZ):
            for cap in range(CAP):
                slot = j * CAP + cap
                out_ref[d, slot] = blocks[j][rows_ref[d * SLOTS + slot]]
        if extra:
            out_ref[d, SLOTS] = refs[9][d]
        return carry

    lax.fori_loop(0, PEERS, step, 0, unroll=2)


def subgrid_kernel(
    tags_ref, left_ref, right_ref, first_ref, second_ref, slabs_ref, out_ref,
    acc_ref, twin_ref, row_ref, tile_ref,
):
    acc_ref[...] = jnp.zeros(acc_ref.shape, F32)

    def embed(i, carry):
        tag = tags_ref[i]
        source = i // SLOTS
        slot = i % SLOTS
        for q in range(NX):
            rows = pl.ds(q * QUARTER, QUARTER)
            acc_ref[tag, rows, :] += slabs_ref[source * NX + q, slot].astype(F32)
        return carry

    lax.fori_loop(0, SOURCES * SLOTS, embed, 0, unroll=4)

    for t in range(SIDE):
        cols = pl.ds(t * LANES, LANES)
        panel = acc_ref[t * SIDE : (t + 1) * SIDE].reshape(SUB, LANES)
        turned = swap_halves(panel)
        twin_ref[:SUB, cols] = panel.astype(BF)
        twin_ref[SUB:, cols] = jnp.where(low_half(panel.shape), -turned, turned).astype(BF)

    step = 2 * LANES
    count = 2 * SUB // step
    for n in range(count):
        cols = pl.ds(n * step, step)
        row_ref[:, cols] = jnp.dot(
            left_ref[...], twin_ref[:, cols], preferred_element_type=F32
        ).astype(BF)
    for n in range(count):
        cols = pl.ds(n * step, step)
        half = pl.ds(n * LANES, LANES)
        got = jnp.dot(row_ref[...], right_ref[:, cols], preferred_element_type=F32)
        real, imag = got[:, :LANES], got[:, LANES:]
        screen_real = first_ref[0, :, half].astype(F32)
        screen_imag = first_ref[1, :, half].astype(F32)
        new_real = (real * screen_real - imag * screen_imag).astype(BF)
        new_imag = (real * screen_imag + imag * screen_real).astype(BF)
        lower = pl.ds(n * step, LANES)
        upper = pl.ds(n * step + LANES, LANES)
        twin_ref[:SUB, lower] = new_real
        twin_ref[:SUB, upper] = new_imag
        twin_ref[SUB:, lower] = new_imag
        twin_ref[SUB:, upper] = -new_real
    for n in range(count):
        cols = pl.ds(n * step, step)
        row_ref[:, cols] = jnp.dot(
            left_ref[...], twin_ref[:, cols], preferred_element_type=F32
        ).astype(BF)
    tile_ref[TILES] = jnp.zeros((WIN, LANES), BF)
    for n in range(count):
        got = lax.dot_general(
            row_ref[...],
            right_ref[pl.ds(n * step, step), :],
            (((1,), (1,)), ((), ())),
            preferred_element_type=F32,
        )
        cols = pl.ds(n * LANES, LANES)
        screen_real = second_ref[0, :, cols].astype(F32)
        screen_imag = second_ref[1, :, cols].astype(F32)
        real_turned, imag_turned = swap_halves(screen_real), swap_halves(screen_imag)
        low = low_half(screen_real.shape)
        for h in range(2):
            part = got[:, h * LANES : (h + 1) * LANES]
            if h == 0:
                keep = jnp.where(low, screen_real, real_turned)
                cross = jnp.where(low, -screen_imag, imag_turned)
            else:
                keep = jnp.where(low, real_turned, screen_real)
                cross = jnp.where(low, -imag_turned, screen_imag)
            done = (part * keep + swap_halves(part) * cross).astype(BF)
            t = 2 * n + h
            tile_ref[t * SIDE : (t + 1) * SIDE] = done.reshape(SIDE, WIN, LANES)

    def cut(i, carry):
        tag = tags_ref[i]
        source = i // SLOTS
        slot = i % SLOTS
        for q in range(NX):
            out_ref[source * NX + q, slot] = tile_ref[tag, pl.ds(q * QUARTER, QUARTER), :]
        return carry

    lax.fori_loop(0, SOURCES * SLOTS, cut, 0, unroll=4)


def add_slots(rows_ref, slots_ref, accs):
    def step(d, carry):
        for cap in range(CAP):
            for j in range(NZ):
                slot = j * CAP + cap
                row = rows_ref[d * SLOTS + slot]
                accs[j][row] += slots_ref[d, slot].astype(F32)
        return carry

    lax.fori_loop(0, PEERS, step, 0)


def sum_first_kernel(rows_ref, slots_ref, *accs):
    for acc in accs:
        acc[...] = jnp.zeros(acc.shape, F32)
    add_slots(rows_ref, slots_ref, accs)


def sum_second_kernel(rows_ref, slots_ref, *refs):
    before, outs, accs = refs[:NZ], refs[NZ : 2 * NZ], refs[2 * NZ :]
    for acc, start in zip(accs, before):
        acc[...] = start[...]
    add_slots(rows_ref, slots_ref, accs)
    for acc, out in zip(accs, outs):
        out[...] = acc[:WIN].astype(BF)


def last_kernel(where_ref, table_ref, *refs):
    blocks, out_ref, tile_ref = refs[:NX], refs[NX], refs[NX + 1]
    count = WIN // NX
    for s in range(NX):
        q = (where_ref[0] + NX - s) % NX
        rows = pl.ds(pl.multiple_of(q * QUARTER, QUARTER), QUARTER)
        for w in range(count):
            tile_ref[w, rows, :] = blocks[s][w].astype(F32)
    for j in range(count // 2):
        ends = []
        for h in range(2):
            both = jnp.dot(
                table_ref[...],
                tile_ref[2 * j + h],
                precision=lax.Precision.HIGHEST,
                preferred_element_type=F32,
            )
            turned = swap_halves(both[WIN:])
            ends.append(both[:WIN] + jnp.where(low_half(turned.shape), -turned, turned))
        even, odd = ends
        low = low_half(even.shape)
        cols = pl.ds(j * LANES, LANES)
        out_ref[0, :, cols] = jnp.where(low, even, swap_halves(odd))
        out_ref[1, :, cols] = jnp.where(low, swap_halves(even), odd)


VMEM = pl.BlockSpec(memory_space=pltpu.VMEM)
SMEM = pl.BlockSpec(memory_space=pltpu.SMEM)


def call(kernel, specs, out, scratch=(), flops=0, moved=0):
    outs = jax.tree.map(lambda _: VMEM, out)
    return pl.pallas_call(
        kernel,
        in_specs=list(specs),
        out_specs=outs,
        out_shape=out,
        scratch_shapes=list(scratch),
        cost_estimate=pl.CostEstimate(flops=flops, bytes_accessed=moved, transcendentals=0),
        compiler_params=pltpu.CompilerParams(vmem_limit_bytes=48 << 20),
    )


def slot_codes(owners, live, place):
    owner, used, tile = owners.reshape(-1), live.reshape(-1), place.reshape(-1)
    entries = owner.shape[0]
    order = jnp.arange(entries, dtype=jnp.int32)
    earlier = (owner[:, None] == owner[None, :]) & (order[:, None] < order[None, :])
    rank = jnp.sum(earlier.astype(jnp.int32), axis=0)
    slot_of = owner * CAP + rank
    code = (order // 3) * TILES + tile + 1
    slots = jnp.arange(NZ * SOURCES * LOCAL * CAP, dtype=jnp.int32)
    hit = (slot_of[None, :] == slots[:, None]) & (used[None, :] == 1)
    return jnp.sum(jnp.where(hit, code[None, :], 0), axis=1) - 1


def shift(value, axis, by):
    size = lax.axis_size(axis)
    return lax.ppermute(value, axis, [(i, (i + by) % size) for i in range(size)])


def pick(rows, index):
    hit = index[:, None] == jnp.arange(rows.shape[0], dtype=jnp.int32)[None, :]
    return jnp.sum(jnp.where(hit[:, :, None], rows[None], 0), axis=1)


def flip(value, axis, bit):
    size = lax.axis_size(axis)
    return lax.ppermute(value, axis, [(i, i ^ bit) for i in range(size)])


def exchange_codes(codes, z, x):
    table = codes.reshape(1, -1)
    for bit in (1, 2, 4):
        other = flip(table, "z", bit)
        table = jnp.concatenate([table, other], 0)
    table = lax.dynamic_index_in_dim(table.reshape(NZ, NZ, -1), z, 1, keepdims=False)
    table = pick(table, (z + jnp.arange(NZ, dtype=jnp.int32)) % NZ ^ z).reshape(1, -1)
    for bit in (1, 2):
        other = flip(table, "x", bit)
        table = jnp.concatenate([table, other], 0)
    table = pick(table, jnp.arange(NX, dtype=jnp.int32) ^ x)
    return table.reshape(NX, NZ, SOURCES, LOCAL, CAP)


def gather_up(own):
    half = WIN // 2
    down, up = [own], [own]
    for _ in range(3):
        up.append(shift(up[-1], "z", 1))
        down.append(shift(down[-1], "z", -1))
    low = shift(up[3][:half], "z", 1)
    high = shift(down[3][half:], "z", -1)
    return down + up[:0:-1] + [low, high]


def add(*terms):
    return sum(t.astype(F32) for t in terms).astype(BF)


def sum_up(parts):
    half = WIN // 2
    low = shift(parts[4][:half], "z", 1)
    high = shift(parts[4][half:], "z", -1)
    up = jnp.concatenate([add(parts[3][:half], low), parts[3][half:]], 0)
    down = jnp.concatenate([parts[5][:half], add(parts[5][half:], high)], 0)
    up, down = shift(up, "z", 1), shift(down, "z", -1)
    up, down = shift(add(parts[2], up), "z", 1), shift(add(parts[6], down), "z", -1)
    up, down = shift(add(parts[1], up), "z", 1), shift(add(parts[7], down), "z", -1)
    return add(parts[0], up, down)


def work(strip, screen_first, screen_second, owners, live, place):
    z, x = lax.axis_index("z"), lax.axis_index("x")
    plane = ("y", "k", "x")
    block = jax.ShapeDtypeStruct((WIN, QUARTER, LANES), BF)
    own = call(
        front_kernel, [SMEM, VMEM, VMEM], block, flops=2 * 32 * 128 * 4096, moved=2 << 20
    )(x.reshape(1), jnp.asarray(front_table()), strip)
    blocks = gather_up(own)

    codes = exchange_codes(slot_codes(owners[0], live[0], place[0]), z, x)
    codes = codes.transpose(3, 2, 0, 1, 4)
    dead = codes < 0
    rows = jnp.where(dead, WIN, codes // TILES).reshape(LOCAL, PEERS * SLOTS)
    taken = jnp.minimum(rows, WIN - 1)
    tags = codes % TILES
    tags = jnp.where(dead, TILES, tags % SIDE * SIDE + tags // SIDE)
    tags = tags.reshape(LOCAL, PEERS, SLOTS).transpose(1, 0, 2).reshape(PEERS, 1, LOCAL * SLOTS)
    extra = jnp.pad(tags.astype(BF), ((0, 0), (0, QUARTER - 1), (0, LANES - LOCAL * SLOTS)))

    left, right = jnp.asarray(left_table()), jnp.asarray(right_table())
    returned = []
    for part in range(LOCAL):
        first = part == 0
        sent = call(
            functools.partial(pack_kernel, first),
            [SMEM] + [VMEM] * (10 if first else 9),
            jax.ShapeDtypeStruct((PEERS, SLOTS + first, QUARTER, LANES), BF),
            scratch=[pltpu.VMEM((WIN, QUARTER, LANES), BF)],
            flops=1 << 28,
            moved=4 << 20,
        )(taken[part], *blocks, *([extra] if first else []))
        got = lax.all_to_all(sent, plane, split_axis=0, concat_axis=0, tiled=True)
        if first:
            spots = got.reshape(SOURCES, NX, SLOTS + 1, QUARTER, LANES)
            spots = spots[:, 0, SLOTS, 0, : LOCAL * SLOTS].astype(jnp.int32)
            spots = spots.reshape(SOURCES, LOCAL, SLOTS).transpose(1, 0, 2)
            spots = spots.reshape(LOCAL, SOURCES * SLOTS)
        done = call(
            subgrid_kernel,
            [SMEM] + [VMEM] * 5,
            jax.ShapeDtypeStruct((PEERS, SLOTS, QUARTER, LANES), BF),
            scratch=[
                pltpu.VMEM((TILES + 1, WIN, LANES), F32),
                pltpu.VMEM((2 * SUB, 2 * SUB), BF),
                pltpu.VMEM((SUB, 2 * SUB), BF),
                pltpu.VMEM((TILES + 1, WIN, LANES), BF),
            ],
            flops=8 * 2 * SUB * SUB * SUB * 2,
            moved=10 << 20,
        )(spots[part], left, right, screen_first, screen_second, got)
        returned.append(lax.all_to_all(done, plane, split_axis=0, concat_axis=0, tiled=True))
    acc = [jax.ShapeDtypeStruct((WIN + 1, QUARTER, LANES), F32)] * NZ
    partial = call(
        sum_first_kernel, [SMEM, VMEM], acc, flops=1 << 28, moved=6 << 20
    )(rows[0], returned[0])
    parts = call(
        sum_second_kernel,
        [SMEM, VMEM] + [VMEM] * NZ,
        [block] * NZ,
        scratch=[pltpu.VMEM((WIN + 1, QUARTER, LANES), F32)] * NZ,
        flops=1 << 28,
        moved=8 << 20,
    )(rows[1], returned[1], *partial)
    mine = sum_up(parts)
    count = WIN // NX
    pieces = []
    for s in range(NX):
        piece = lax.dynamic_slice_in_dim(mine, (x + s) % NX * count, count, 0)
        pieces.append(shift(piece, "x", s) if s else piece)
    return call(
        last_kernel,
        [SMEM] + [VMEM] * (1 + NX),
        jax.ShapeDtypeStruct((2, WIN, count * WIN), F32),
        scratch=[pltpu.VMEM((count, WIN, LANES), F32)],
        flops=1 << 28,
        moved=1 << 20,
    )(x.reshape(1), jnp.asarray(last_table()), *pieces)


def solution(mesh):
    fine = Mesh(mesh.devices.reshape(NZ, NY, NK, NX), ("z", "y", "k", "x"))
    facet = ("z", "y", "k")
    entry = P("x", facet, None)
    return jax.shard_map(
        work,
        mesh=fine,
        in_specs=(P(None, None, facet), P(), P(), entry, entry, entry),
        out_specs=P(None, None, facet + ("x",)),
        check_vma=False,
    )
```

time: 502 us -> 245 us (0.49); the launches traced: 492 us -> 243 us
  matrix products: 175 us -> 0 us
  blocking collectives: 84.4 us -> 0 us
  local copies, waits for them, and re-layouts: 76.4 us -> 11.3 us
  Pallas kernels: 0 us -> 35.6 us
  waiting for transfers between devices: 99.1 us -> 126 us
  starting transfers between devices: 41.7 us -> 67.1 us
  other arithmetic: 14.8 us -> 2.7 us
    dot_general x46 -> x0, matrix products: 175 us -> none  [the longest x4 21 us: right_apply(): jnp.dot(imag_part, real_table, preferred_element_type=jnp.float32)]
    all_to_all x2 -> x0, blocking collectives: 84.4 us -> none  [the longest x1 65.1 us: exchange_in_groups(): lax.all_to_all(group, axis, split_axis=split_dim, concat_axis=concat_dim,...]
    ppermute x0 -> x24, starting transfers between devices: none -> 47 us  [the longest x19 32.3 us: shift(): lax.ppermute(value, axis, [(i, (i + by) % size) for i in range(size)])]
    ppermute x0 -> x24, waiting for transfers between devices: none -> 45.5 us  [the longest x19 38.4 us: shift(): lax.ppermute(value, axis, [(i, (i + by) % size) for i in range(size)])]
    pallas_call x0 -> x8, Pallas kernels: none -> 35.6 us  [the longest x2 22.4 us: work(): call(subgrid_kernel, [SMEM] + [VMEM] * 5, jax.ShapeDtypeStruct((PEERS, SL...]
    reshape x9 -> x2, local copies, waits for them, and re-layouts: 30.6 us -> 0.39 us  [the longest x1 0.31 us: exchange_codes(): return table.reshape(NX, NZ, SOURCES, LOCAL, CAP)]
    all_to_all x5 -> x4, starting transfers between devices: 41.7 us -> 20.1 us  [the longest x2 10.5 us: work(): got = lax.all_to_all(sent, plane, split_axis=0, concat_axis=0, tiled=True)]
    all_to_all x5 -> x4, waiting for transfers between devices: 99.1 us -> 80.4 us  [the longest x2 41.4 us: work(): got = lax.all_to_all(sent, plane, split_axis=0, concat_axis=0, tiled=True)]
  transfers between devices with their start and end apart: 5 -> 28, of which waited for: 4 -> 22; matrix products, arithmetic and copies ran while one was open for 17% -> 3% of each run, Pallas kernels for 0% -> 12%
where the time goes in v1:
time: 245 us; the launch traced here: 243 us
  waiting for transfers between devices  126 us (51%)
  starting transfers between devices  67.1 us (27%)
  Pallas kernels  35.6 us (15%)
  local copies, waits for them, and re-layouts  11.3 us (5%)
  other arithmetic  2.7 us (1%)
    all_to_all x2, waiting for transfers between devices, work(): got = lax.all_to_all(sent, plane, split_axis=0, concat_axis=0, tiled=True)  41.4 us
    all_to_all x2, waiting for transfers between devices, work(): lax.all_to_all(done, plane, split_axis=0, concat_axis=0, tiled=True)  39 us
    ppermute x19, waiting for transfers between devices, shift(): lax.ppermute(value, axis, [(i, (i + by) % size) for i in range(size)])  38.4 us
    ppermute x19, starting transfers between devices, shift(): lax.ppermute(value, axis, [(i, (i + by) % size) for i in range(size)])  32.3 us
    pallas_call x2, Pallas kernels, work(): call(subgrid_kernel, [SMEM] + [VMEM] * 5, jax.ShapeDtypeStruct((PEERS, SL...  22.4 us
    ppermute x5, starting transfers between devices, flip(): return lax.ppermute(value, axis, [(i, i ^ bit) for i in range(size)])  14.7 us
    all_to_all x2, starting transfers between devices, work(): got = lax.all_to_all(sent, plane, split_axis=0, concat_axis=0, tiled=True)  10.5 us
    all_to_all x2, starting transfers between devices, work(): lax.all_to_all(done, plane, split_axis=0, concat_axis=0, tiled=True)  9.57 us
  transfers between devices with their start and end apart: 28, of which 22 were waited for; matrix products, arithmetic and copies ran while one was open for 3% of the time, Pallas kernels for 12%

profile of v1, /device:TPU:32, one launch (start us, length us, event | category | flops | bytes accessed | tf_op | source)
XLA Modules:
  0.0 242.9 jit_solution(7892481391265369169)
XLA Ops:
  9.6 3.7 %collective-permute-start.1 = (s32[2,256]{1,0:T(2,128)S(1)}, s32[2,256]{1,0:T(2,128)S(1)}, u32[]{:S(2)}, u32[]{:S(2)}) collective-permute-start(s32[2,256]{1,0:T(2,128)S(1)} %pad_add_fusion.2), channel_id=1, source_target_pairs={{0,64},{32,96},{64,0},{96,32},{128,192},{160,224},{192,128},{224,1... | collective-permute-start | bytes 6152 | tf_op jit(solution)/shard_map/ppermute | solution.py:286
  13.3 3.5 %collective-permute-done.1 = s32[2,256]{1,0:T(2,128)S(1)} collective-permute-done((s32[2,256]{1,0:T(2,128)S(1)}, s32[2,256]{1,0:T(2,128)S(1)}, u32[]{:S(2)}, u32[]{:S(2)}) %collective-permute-start.1) | collective-permute-done | bytes 2080 | tf_op jit(solution)/shard_map/ppermute | solution.py:286
  16.8 4.6 %collective-permute-start.2 = (s32[4,256]{1,0:T(4,128)S(1)}, s32[4,256]{1,0:T(4,128)S(1)}, u32[]{:S(2)}, u32[]{:S(2)}) collective-permute-start(s32[4,256]{1,0:T(4,128)S(1)} %pad_add_fusion), channel_id=1, source_target_pairs={{0,128},{32,160},{64,192},{96,224},{128,0},{160,32},{192,64},{224,... | collective-permute-start | bytes 12296 | tf_op jit(solution)/shard_map/ppermute | solution.py:286
  34.6 6.2 %collective-permute-done.6.refs_2_ = bf16[64,16,128]{2,1,0:T(8,128)(2,1)S(1)} collective-permute-done((bf16[64,16,128]{2,1,0:T(8,128)(2,1)S(1)}, bf16[64,16,128]{2,1,0:T(8,128)(2,1)S(1)}, u32[]{:S(2)}, u32[]{:S(2)}) %collective-permute-start.6) | collective-permute-done | bytes 262176 | tf_op jit(solution)/shard_map/ppermute | solution.py:276
  43.8 7.3 %collective-permute-done.10.refs_4_ = bf16[64,16,128]{2,1,0:T(8,128)(2,1)S(1)} collective-permute-done((bf16[64,16,128]{2,1,0:T(8,128)(2,1)S(1)}, bf16[64,16,128]{2,1,0:T(8,128)(2,1)S(1)}, u32[]{:S(2)}, u32[]{:S(2)}) %collective-permute-start.10) | collective-permute-done | bytes 262176 | tf_op jit(solution)/shard_map/ppermute | solution.py:276
  51.3 3.3 %collective-permute-start.12 = (bf16[32,16,128]{2,1,0:T(8,128)(2,1)S(1)}, bf16[32,16,128]{2,1,0:T(8,128)(2,1)S(1)}, u32[]{:S(2)}, u32[]{:S(2)}) collective-permute-start(bf16[32,16,128]{2,1,0:T(8,128)(2,1)S(1)} %slice.69), channel_id=1, source_target_pairs={{0,224},{32,0},{64,32},{96,64},{128,96},{160,128},{192,160},{224,1... | collective-permute-start | bytes 393224 | tf_op jit(solution)/shard_map/ppermute | solution.py:276
  60.0 5.6 %all-to-all-start = ((bf16[32,17,16,128]{3,2,1,0:T(8,128)(2,1)}), bf16[32,17,16,128]{3,2,1,0:T(8,128)(2,1)}, u32[]{:S(2)}, u32[]{:S(2)}) async-start(bf16[32,17,16,128]{3,2,1,0:T(8,128)(2,1)} %shard_map.101), calls=%async_computation | async-start | bytes 4456448 | tf_op jit(solution)/shard_map/all_to_all | solution.py:361
  68.5 25.9 %all-to-all-done.slabs_ref = bf16[32,17,16,128]{3,2,1,0:T(8,128)(2,1)} async-done(((bf16[32,17,16,128]{3,2,1,0:T(8,128)(2,1)}), bf16[32,17,16,128]{3,2,1,0:T(8,128)(2,1)}, u32[]{:S(2)}, u32[]{:S(2)}) %all-to-all-start) | async-done | bytes 2228256 | tf_op jit(solution)/shard_map/all_to_all | solution.py:361
  94.5 4.9 %all-to-all-start.1 = ((bf16[32,16,16,128]{3,2,1,0:T(8,128)(2,1)}), bf16[32,16,16,128]{3,2,1,0:T(8,128)(2,1)}, u32[]{:S(2)}, u32[]{:S(2)}) async-start(bf16[32,16,16,128]{3,2,1,0:T(8,128)(2,1)} %shard_map.102), calls=%async_computation.1 | async-start | bytes 4194304 | tf_op jit(solution)/shard_map/all_to_all | solution.py:361
  100.3 11.2 %shard_map.104 = bf16[32,16,16,128]{3,2,1,0:T(8,128)(2,1)} custom-call(s32[128]{0:T(128)S(1)} %squeeze.26.tags_ref, bf16[512,1024]{1,0:T(8,128)(2,1)S(1)} %copy-done.7, bf16[1024,1024]{1,0:T(8,128)(2,1)} %constant.127.clone.right_ref, bf16[2,512,512]{2,1,0:T(8,128)(2,1)S(1)} %copy-done.5, bf16[2,512,512]{2,1,0:T(8,128)(2,1)S(1)} %copy-done.6, ...), custom_call_target="tpu_custom_call" | custom-call | flops 4294967296 | bytes 10485760 | tf_op jit(solution)/shard_map/pallas_call | solution.py:367
  111.6 15.5 %all-to-all-done.1.slabs_ref = bf16[32,16,16,128]{3,2,1,0:T(8,128)(2,1)} async-done(((bf16[32,16,16,128]{3,2,1,0:T(8,128)(2,1)}), bf16[32,16,16,128]{3,2,1,0:T(8,128)(2,1)}, u32[]{:S(2)}, u32[]{:S(2)}) %all-to-all-start.1) | async-done | bytes 2097184 | tf_op jit(solution)/shard_map/all_to_all | solution.py:361
  127.1 4.8 %all-to-all-start.3 = ((bf16[32,16,16,128]{3,2,1,0:T(8,128)(2,1)}), bf16[32,16,16,128]{3,2,1,0:T(8,128)(2,1)}, u32[]{:S(2)}, u32[]{:S(2)}) async-start(bf16[32,16,16,128]{3,2,1,0:T(8,128)(2,1)} %shard_map.104), calls=%async_computation.3 | async-start | bytes 4194304 | tf_op jit(solution)/shard_map/all_to_all | solution.py:380
  131.9 11.2 %shard_map.103 = bf16[32,16,16,128]{3,2,1,0:T(8,128)(2,1)} custom-call(s32[128]{0:T(128)S(1)} %squeeze.23.tags_ref, bf16[512,1024]{1,0:T(8,128)(2,1)S(1)} %copy-done.7, bf16[1024,1024]{1,0:T(8,128)(2,1)} %constant.127.clone.right_ref, bf16[2,512,512]{2,1,0:T(8,128)(2,1)S(1)} %copy-done.5, bf16[2,512,512]{2,1,0:T(8,128)(2,1)S(1)} %copy-done.6, ...), custom_call_target="tpu_custom_call" | custom-call | flops 4294967296 | bytes 10485760 | tf_op jit(solution)/shard_map/pallas_call | solution.py:367
  143.1 16.4 %all-to-all-done.3.slots_ref = bf16[32,16,16,128]{3,2,1,0:T(8,128)(2,1)} async-done(((bf16[32,16,16,128]{3,2,1,0:T(8,128)(2,1)}), bf16[32,16,16,128]{3,2,1,0:T(8,128)(2,1)}, u32[]{:S(2)}, u32[]{:S(2)}) %all-to-all-start.3) | async-done | bytes 2097184 | tf_op jit(solution)/shard_map/all_to_all | solution.py:380
  159.5 4.8 %all-to-all-start.2 = ((bf16[32,16,16,128]{3,2,1,0:T(8,128)(2,1)}), bf16[32,16,16,128]{3,2,1,0:T(8,128)(2,1)}, u32[]{:S(2)}, u32[]{:S(2)}) async-start(bf16[32,16,16,128]{3,2,1,0:T(8,128)(2,1)} %shard_map.103), calls=%async_computation.2 | async-start | bytes 4194304 | tf_op jit(solution)/shard_map/all_to_all | solution.py:380
  169.4 22.6 %all-to-all-done.2.slots_ref = bf16[32,16,16,128]{3,2,1,0:T(8,128)(2,1)} async-done(((bf16[32,16,16,128]{3,2,1,0:T(8,128)(2,1)}), bf16[32,16,16,128]{3,2,1,0:T(8,128)(2,1)}, u32[]{:S(2)}, u32[]{:S(2)}) %all-to-all-start.2) | async-done | bytes 2097184 | tf_op jit(solution)/shard_map/all_to_all | solution.py:380
  196.1 3.5 %collective-permute-start.17 = (bf16[32,16,128]{2,1,0:T(8,128)(2,1)S(1)}, bf16[32,16,128]{2,1,0:T(8,128)(2,1)S(1)}, u32[]{:S(2)}, u32[]{:S(2)}) collective-permute-start(bf16[32,16,128]{2,1,0:T(8,128)(2,1)S(1)} %get-tuple-element.46), channel_id=1, source_target_pairs={{0,224},{32,0},{64,32},{96,64},{128,96},{160,128},{192,160},{224,1... | collective-permute-start | bytes 393224 | tf_op jit(solution)/shard_map/ppermute | solution.py:276
  202.2 3.4 %collective-permute-start.18 = (bf16[64,16,128]{2,1,0:T(8,128)(2,1)S(1)}, bf16[64,16,128]{2,1,0:T(8,128)(2,1)S(1)}, u32[]{:S(2)}, u32[]{:S(2)}) collective-permute-start(bf16[64,16,128]{2,1,0:T(8,128)(2,1)S(1)} %pad_maximum_fusion.1), channel_id=1, source_target_pairs={{0,224},{32,0},{64,32},{96,64},{128,96},{160,128},{192,160},{224,1... | collective-permute-start | bytes 786440 | tf_op jit(solution)/shard_map/ppermute | solution.py:276
  206.1 3.7 %collective-permute-done.18 = bf16[64,16,128]{2,1,0:T(8,128)(2,1)S(1)} collective-permute-done((bf16[64,16,128]{2,1,0:T(8,128)(2,1)S(1)}, bf16[64,16,128]{2,1,0:T(8,128)(2,1)S(1)}, u32[]{:S(2)}, u32[]{:S(2)}) %collective-permute-start.18) | collective-permute-done | bytes 262176 | tf_op jit(solution)/shard_map/ppermute | solution.py:276
  209.9 3.4 %collective-permute-start.19 = (bf16[64,16,128]{2,1,0:T(8,128)(2,1)S(1)}, bf16[64,16,128]{2,1,0:T(8,128)(2,1)S(1)}, u32[]{:S(2)}, u32[]{:S(2)}) collective-permute-start(bf16[64,16,128]{2,1,0:T(8,128)(2,1)S(1)} %add_convert_fusion.2), channel_id=1, source_target_pairs={{0,224},{32,0},{64,32},{96,64},{128,96},{160,128},{192,160},{224,1... | collective-permute-start | bytes 786440 | tf_op jit(solution)/shard_map/ppermute | solution.py:276
  213.9 3.3 %collective-permute-done.19 = bf16[64,16,128]{2,1,0:T(8,128)(2,1)S(1)} collective-permute-done((bf16[64,16,128]{2,1,0:T(8,128)(2,1)S(1)}, bf16[64,16,128]{2,1,0:T(8,128)(2,1)S(1)}, u32[]{:S(2)}, u32[]{:S(2)}) %collective-permute-start.19) | collective-permute-done | bytes 262176 | tf_op jit(solution)/shard_map/ppermute | solution.py:276
  217.3 3.8 %collective-permute-start.20 = (bf16[64,16,128]{2,1,0:T(8,128)(2,1)S(1)}, bf16[64,16,128]{2,1,0:T(8,128)(2,1)S(1)}, u32[]{:S(2)}, u32[]{:S(2)}) collective-permute-start(bf16[64,16,128]{2,1,0:T(8,128)(2,1)S(1)} %add_convert_fusion.1), channel_id=1, source_target_pairs={{0,224},{32,0},{64,32},{96,64},{128,96},{160,128},{192,160},{224,1... | collective-permute-start | bytes 786440 | tf_op jit(solution)/shard_map/ppermute | solution.py:276
  224.9 4.5 %collective-permute-done.16 = bf16[64,16,128]{2,1,0:T(8,128)(2,1)S(1)} collective-permute-done((bf16[64,16,128]{2,1,0:T(8,128)(2,1)S(1)}, bf16[64,16,128]{2,1,0:T(8,128)(2,1)S(1)}, u32[]{:S(2)}, u32[]{:S(2)}) %collective-permute-start.16) | collective-permute-done | bytes 262176 | tf_op jit(solution)/shard_map/ppermute | solution.py:276
  231.6 5.0 %collective-permute-start.22 = (bf16[16,16,128]{2,1,0:T(8,128)(2,1)S(1)}, bf16[16,16,128]{2,1,0:T(8,128)(2,1)S(1)}, u32[]{:S(2)}, u32[]{:S(2)}) collective-permute-start(bf16[16,16,128]{2,1,0:T(8,128)(2,1)S(1)} %get-tuple-element.42), channel_id=1, source_target_pairs={{0,2},{1,3},{2,0},{3,1},{4,6},{5,7},{6,4},{7,5},{8,10},{9,11},{10,... | collective-permute-start | bytes 196616 | tf_op jit(solution)/shard_map/ppermute | solution.py:276
  (125 shorter events, 60.6 us)
Async XLA Ops:
  3.1 6.5 %collective-permute-start = (s32[1,256]{1,0:T(1,128)S(1)}, s32[1,256]{1,0:T(1,128)S(1)}, u32[]{:S(2)}, u32[]{:S(2)}) collective-permute-start(s32[1,256]{1,0:T(1,128)S(1)} %bitcast.50), channel_id=1, source_target_pairs={{0,32},{32,0},{64,96},{96,64},{128,160},{160,128},{192,224},{224,1... | collective-permute-start | bytes 3080 | tf_op jit(solution)/shard_map/ppermute | solution.py:286
  7.4 23.8 %collective-permute-start.5 = (bf16[64,16,128]{2,1,0:T(8,128)(2,1)S(1)}, bf16[64,16,128]{2,1,0:T(8,128)(2,1)S(1)}, u32[]{:S(2)}, u32[]{:S(2)}) collective-permute-start(bf16[64,16,128]{2,1,0:T(8,128)(2,1)S(1)} %shard_map.100.refs_0_), channel_id=1, source_target_pairs={{0,224},{32,0},{64,32},{96,64},{128,96},{160,128},{192,160},{224,1... | collective-permute-start | bytes 786440 | tf_op jit(solution)/shard_map/ppermute | solution.py:276
  7.7 24.7 %collective-permute-start.8 = (bf16[64,16,128]{2,1,0:T(8,128)(2,1)S(1)}, bf16[64,16,128]{2,1,0:T(8,128)(2,1)S(1)}, u32[]{:S(2)}, u32[]{:S(2)}) collective-permute-start(bf16[64,16,128]{2,1,0:T(8,128)(2,1)S(1)} %shard_map.100.refs_0_), channel_id=1, source_target_pairs={{0,32},{32,64},{64,96},{96,128},{128,160},{160,192},{192,224},{224... | collective-permute-start | bytes 786440 | tf_op jit(solution)/shard_map/ppermute | solution.py:276
  9.6 7.1 %collective-permute-start.1 = (s32[2,256]{1,0:T(2,128)S(1)}, s32[2,256]{1,0:T(2,128)S(1)}, u32[]{:S(2)}, u32[]{:S(2)}) collective-permute-start(s32[2,256]{1,0:T(2,128)S(1)} %pad_add_fusion.2), channel_id=1, source_target_pairs={{0,64},{32,96},{64,0},{96,32},{128,192},{160,224},{192,128},{224,1... | collective-permute-start | bytes 6152 | tf_op jit(solution)/shard_map/ppermute | solution.py:286
  16.8 7.6 %collective-permute-start.2 = (s32[4,256]{1,0:T(4,128)S(1)}, s32[4,256]{1,0:T(4,128)S(1)}, u32[]{:S(2)}, u32[]{:S(2)}) collective-permute-start(s32[4,256]{1,0:T(4,128)S(1)} %pad_add_fusion), channel_id=1, source_target_pairs={{0,128},{32,160},{64,192},{96,224},{128,0},{160,32},{192,64},{224,... | collective-permute-start | bytes 12296 | tf_op jit(solution)/shard_map/ppermute | solution.py:286
  28.2 6.3 %collective-permute-start.4 = (s32[2,256]{1,0:T(2,128)S(1)}, s32[2,256]{1,0:T(2,128)S(1)}, u32[]{:S(2)}, u32[]{:S(2)}) collective-permute-start(s32[2,256]{1,0:T(2,128)S(1)} %pad_add_fusion.3), channel_id=1, source_target_pairs={{0,2},{1,3},{2,0},{3,1},{4,6},{5,7},{6,4},{7,5},{8,10},{9,11},{10,... | collective-permute-start | bytes 6152 | tf_op jit(solution)/shard_map/ppermute | solution.py:286
  31.3 9.5 %collective-permute-start.6 = (bf16[64,16,128]{2,1,0:T(8,128)(2,1)S(1)}, bf16[64,16,128]{2,1,0:T(8,128)(2,1)S(1)}, u32[]{:S(2)}, u32[]{:S(2)}) collective-permute-start(bf16[64,16,128]{2,1,0:T(8,128)(2,1)S(1)} %collective-permute-done.5.refs_1_), channel_id=1, source_target_pairs={{0,224},{32,0},{64,32},{96,64},{128,96},{160,128},{192,160},{224,1... | collective-permute-start | bytes 786440 | tf_op jit(solution)/shard_map/ppermute | solution.py:276
  32.4 9.5 %collective-permute-start.9 = (bf16[64,16,128]{2,1,0:T(8,128)(2,1)S(1)}, bf16[64,16,128]{2,1,0:T(8,128)(2,1)S(1)}, u32[]{:S(2)}, u32[]{:S(2)}) collective-permute-start(bf16[64,16,128]{2,1,0:T(8,128)(2,1)S(1)} %collective-permute-done.8.refs_6_), channel_id=1, source_target_pairs={{0,32},{32,64},{64,96},{96,128},{128,160},{160,192},{192,224},{224... | collective-permute-start | bytes 786440 | tf_op jit(solution)/shard_map/ppermute | solution.py:276
  40.8 10.5 %collective-permute-start.7 = (bf16[64,16,128]{2,1,0:T(8,128)(2,1)S(1)}, bf16[64,16,128]{2,1,0:T(8,128)(2,1)S(1)}, u32[]{:S(2)}, u32[]{:S(2)}) collective-permute-start(bf16[64,16,128]{2,1,0:T(8,128)(2,1)S(1)} %collective-permute-done.6.refs_2_), channel_id=1, source_target_pairs={{0,224},{32,0},{64,32},{96,64},{128,96},{160,128},{192,160},{224,1... | collective-permute-start | bytes 786440 | tf_op jit(solution)/shard_map/ppermute | solution.py:276
  41.9 9.3 %collective-permute-start.10 = (bf16[64,16,128]{2,1,0:T(8,128)(2,1)S(1)}, bf16[64,16,128]{2,1,0:T(8,128)(2,1)S(1)}, u32[]{:S(2)}, u32[]{:S(2)}) collective-permute-start(bf16[64,16,128]{2,1,0:T(8,128)(2,1)S(1)} %collective-permute-done.9.refs_5_), channel_id=1, source_target_pairs={{0,32},{32,64},{64,96},{96,128},{128,160},{160,192},{192,224},{224... | collective-permute-start | bytes 786440 | tf_op jit(solution)/shard_map/ppermute | solution.py:276
  51.2 6.3 %collective-permute-start.11 = (bf16[32,16,128]{2,1,0:T(8,128)(2,1)S(1)}, bf16[32,16,128]{2,1,0:T(8,128)(2,1)S(1)}, u32[]{:S(2)}, u32[]{:S(2)}) collective-permute-start(bf16[32,16,128]{2,1,0:T(8,128)(2,1)S(1)} %slice.68), channel_id=1, source_target_pairs={{0,32},{32,64},{64,96},{96,128},{128,160},{160,192},{192,224},{224... | collective-permute-start | bytes 393224 | tf_op jit(solution)/shard_map/ppermute | solution.py:276
  60.0 34.5 %all-to-all-start = ((bf16[32,17,16,128]{3,2,1,0:T(8,128)(2,1)}), bf16[32,17,16,128]{3,2,1,0:T(8,128)(2,1)}, u32[]{:S(2)}, u32[]{:S(2)}) async-start(bf16[32,17,16,128]{3,2,1,0:T(8,128)(2,1)} %shard_map.101), calls=%async_computation | async-start | bytes 4456448 | tf_op jit(solution)/shard_map/all_to_all | solution.py:361
  94.5 32.6 %all-to-all-start.1 = ((bf16[32,16,16,128]{3,2,1,0:T(8,128)(2,1)}), bf16[32,16,16,128]{3,2,1,0:T(8,128)(2,1)}, u32[]{:S(2)}, u32[]{:S(2)}) async-start(bf16[32,16,16,128]{3,2,1,0:T(8,128)(2,1)} %shard_map.102), calls=%async_computation.1 | async-start | bytes 4194304 | tf_op jit(solution)/shard_map/all_to_all | solution.py:361
  127.1 32.5 %all-to-all-start.3 = ((bf16[32,16,16,128]{3,2,1,0:T(8,128)(2,1)}), bf16[32,16,16,128]{3,2,1,0:T(8,128)(2,1)}, u32[]{:S(2)}, u32[]{:S(2)}) async-start(bf16[32,16,16,128]{3,2,1,0:T(8,128)(2,1)} %shard_map.104), calls=%async_computation.3 | async-start | bytes 4194304 | tf_op jit(solution)/shard_map/all_to_all | solution.py:380
  159.5 32.5 %all-to-all-start.2 = ((bf16[32,16,16,128]{3,2,1,0:T(8,128)(2,1)}), bf16[32,16,16,128]{3,2,1,0:T(8,128)(2,1)}, u32[]{:S(2)}, u32[]{:S(2)}) async-start(bf16[32,16,16,128]{3,2,1,0:T(8,128)(2,1)} %shard_map.103), calls=%async_computation.2 | async-start | bytes 4194304 | tf_op jit(solution)/shard_map/all_to_all | solution.py:380
  199.6 6.3 %collective-permute-start.13 = (bf16[32,16,128]{2,1,0:T(8,128)(2,1)S(1)}, bf16[32,16,128]{2,1,0:T(8,128)(2,1)S(1)}, u32[]{:S(2)}, u32[]{:S(2)}) collective-permute-start(bf16[32,16,128]{2,1,0:T(8,128)(2,1)S(1)} %get-tuple-element.45), channel_id=1, source_target_pairs={{0,32},{32,64},{64,96},{96,128},{128,160},{160,192},{192,224},{224... | collective-permute-start | bytes 393224 | tf_op jit(solution)/shard_map/ppermute | solution.py:276
  202.2 7.6 %collective-permute-start.18 = (bf16[64,16,128]{2,1,0:T(8,128)(2,1)S(1)}, bf16[64,16,128]{2,1,0:T(8,128)(2,1)S(1)}, u32[]{:S(2)}, u32[]{:S(2)}) collective-permute-start(bf16[64,16,128]{2,1,0:T(8,128)(2,1)S(1)} %pad_maximum_fusion.1), channel_id=1, source_target_pairs={{0,224},{32,0},{64,32},{96,64},{128,96},{160,128},{192,160},{224,1... | collective-permute-start | bytes 786440 | tf_op jit(solution)/shard_map/ppermute | solution.py:276
  206.0 7.7 %collective-permute-start.14 = (bf16[64,16,128]{2,1,0:T(8,128)(2,1)S(1)}, bf16[64,16,128]{2,1,0:T(8,128)(2,1)S(1)}, u32[]{:S(2)}, u32[]{:S(2)}) collective-permute-start(bf16[64,16,128]{2,1,0:T(8,128)(2,1)S(1)} %pad_maximum_fusion), channel_id=1, source_target_pairs={{0,32},{32,64},{64,96},{96,128},{128,160},{160,192},{192,224},{224... | collective-permute-start | bytes 786440 | tf_op jit(solution)/shard_map/ppermute | solution.py:276
  209.9 7.3 %collective-permute-start.19 = (bf16[64,16,128]{2,1,0:T(8,128)(2,1)S(1)}, bf16[64,16,128]{2,1,0:T(8,128)(2,1)S(1)}, u32[]{:S(2)}, u32[]{:S(2)}) collective-permute-start(bf16[64,16,128]{2,1,0:T(8,128)(2,1)S(1)} %add_convert_fusion.2), channel_id=1, source_target_pairs={{0,224},{32,0},{64,32},{96,64},{128,96},{160,128},{192,160},{224,1... | collective-permute-start | bytes 786440 | tf_op jit(solution)/shard_map/ppermute | solution.py:276
  213.8 7.7 %collective-permute-start.15 = (bf16[64,16,128]{2,1,0:T(8,128)(2,1)S(1)}, bf16[64,16,128]{2,1,0:T(8,128)(2,1)S(1)}, u32[]{:S(2)}, u32[]{:S(2)}) collective-permute-start(bf16[64,16,128]{2,1,0:T(8,128)(2,1)S(1)} %add_convert_fusion.4), channel_id=1, source_target_pairs={{0,32},{32,64},{64,96},{96,128},{128,160},{160,192},{192,224},{224... | collective-permute-start | bytes 786440 | tf_op jit(solution)/shard_map/ppermute | solution.py:276
  217.3 7.7 %collective-permute-start.20 = (bf16[64,16,128]{2,1,0:T(8,128)(2,1)S(1)}, bf16[64,16,128]{2,1,0:T(8,128)(2,1)S(1)}, u32[]{:S(2)}, u32[]{:S(2)}) collective-permute-start(bf16[64,16,128]{2,1,0:T(8,128)(2,1)S(1)} %add_convert_fusion.1), channel_id=1, source_target_pairs={{0,224},{32,0},{64,32},{96,64},{128,96},{160,128},{192,160},{224,1... | collective-permute-start | bytes 786440 | tf_op jit(solution)/shard_map/ppermute | solution.py:276
  221.6 7.8 %collective-permute-start.16 = (bf16[64,16,128]{2,1,0:T(8,128)(2,1)S(1)}, bf16[64,16,128]{2,1,0:T(8,128)(2,1)S(1)}, u32[]{:S(2)}, u32[]{:S(2)}) collective-permute-start(bf16[64,16,128]{2,1,0:T(8,128)(2,1)S(1)} %add_convert_fusion.3), channel_id=1, source_target_pairs={{0,32},{32,64},{64,96},{96,128},{128,160},{160,192},{192,224},{224... | collective-permute-start | bytes 786440 | tf_op jit(solution)/shard_map/ppermute | solution.py:276
  229.5 7.9 %collective-permute-start.21 = (bf16[16,16,128]{2,1,0:T(8,128)(2,1)S(1)}, bf16[16,16,128]{2,1,0:T(8,128)(2,1)S(1)}, u32[]{:S(2)}, u32[]{:S(2)}) collective-permute-start(bf16[16,16,128]{2,1,0:T(8,128)(2,1)S(1)} %get-tuple-element.43), channel_id=1, source_target_pairs={{0,1},{1,2},{2,3},{3,0},{4,5},{5,6},{6,7},{7,4},{8,9},{9,10},{10,1... | collective-permute-start | bytes 196616 | tf_op jit(solution)/shard_map/ppermute | solution.py:276
  231.6 8.0 %collective-permute-start.22 = (bf16[16,16,128]{2,1,0:T(8,128)(2,1)S(1)}, bf16[16,16,128]{2,1,0:T(8,128)(2,1)S(1)}, u32[]{:S(2)}, u32[]{:S(2)}) collective-permute-start(bf16[16,16,128]{2,1,0:T(8,128)(2,1)S(1)} %get-tuple-element.42), channel_id=1, source_target_pairs={{0,2},{1,3},{2,0},{3,1},{4,6},{5,7},{6,4},{7,5},{8,10},{9,11},{10,... | collective-permute-start | bytes 196616 | tf_op jit(solution)/shard_map/ppermute | solution.py:276
  (13 other events, 151.2 us)

commit v2 on v1

--- a/solution.py
+++ b/solution.py
@@ -80,6 +80,30 @@
         low = low_half(real.shape)
         out_ref[2 * j] = jnp.where(low, real, swap_halves(imag)).astype(BF)
         out_ref[2 * j + 1] = jnp.where(low, swap_halves(real), imag).astype(BF)
+
+
+def codes_kernel(owner_ref, live_ref, place_ref, out_ref):
+    shape = (WIN, NZ * SOURCES * LOCAL)
+    window = lax.broadcasted_iota(jnp.int32, shape, 0)
+    subgrid = lax.broadcasted_iota(jnp.int32, shape, 1)
+    count = jnp.zeros(shape, F32)
+    value = jnp.zeros(shape, F32)
+    for k in range(3):
+        entry = (0, slice(None), slice(k, k + 1))
+        hit = owner_ref[entry] == subgrid
+        code = (window * TILES + place_ref[entry] + 1).astype(F32)
+        count += jnp.where(hit, 1.0, 0.0)
+        value += jnp.where(hit & (live_ref[entry] == 1), code, 0.0)
+    square = (WIN, WIN)
+    earlier = lax.broadcasted_iota(jnp.int32, square, 1) < lax.broadcasted_iota(
+        jnp.int32, square, 0
+    )
+    rank = jnp.dot(
+        jnp.where(earlier, 1.0, 0.0).astype(BF), count.astype(BF), preferred_element_type=F32
+    )
+    for cap in range(CAP):
+        mine = jnp.sum(jnp.where(rank == float(cap), value, 0.0), axis=0, keepdims=True)
+        out_ref[:, cap * shape[1] : (cap + 1) * shape[1]] = mine.astype(jnp.int32) - 1
 
 
 def pack_kernel(extra, rows_ref, *refs):
@@ -258,19 +282,6 @@
     )
 
 
-def slot_codes(owners, live, place):
-    owner, used, tile = owners.reshape(-1), live.reshape(-1), place.reshape(-1)
-    entries = owner.shape[0]
-    order = jnp.arange(entries, dtype=jnp.int32)
-    earlier = (owner[:, None] == owner[None, :]) & (order[:, None] < order[None, :])
-    rank = jnp.sum(earlier.astype(jnp.int32), axis=0)
-    slot_of = owner * CAP + rank
-    code = (order // 3) * TILES + tile + 1
-    slots = jnp.arange(NZ * SOURCES * LOCAL * CAP, dtype=jnp.int32)
-    hit = (slot_of[None, :] == slots[:, None]) & (used[None, :] == 1)
-    return jnp.sum(jnp.where(hit, code[None, :], 0), axis=1) - 1
-
-
 def shift(value, axis, by):
     size = lax.axis_size(axis)
     return lax.ppermute(value, axis, [(i, (i + by) % size) for i in range(size)])
@@ -287,17 +298,18 @@
 
 
 def exchange_codes(codes, z, x):
-    table = codes.reshape(1, -1)
+    table = codes
     for bit in (1, 2, 4):
         other = flip(table, "z", bit)
         table = jnp.concatenate([table, other], 0)
-    table = lax.dynamic_index_in_dim(table.reshape(NZ, NZ, -1), z, 1, keepdims=False)
-    table = pick(table, (z + jnp.arange(NZ, dtype=jnp.int32)) % NZ ^ z).reshape(1, -1)
-    for bit in (1, 2):
-        other = flip(table, "x", bit)
-        table = jnp.concatenate([table, other], 0)
-    table = pick(table, jnp.arange(NX, dtype=jnp.int32) ^ x)
-    return table.reshape(NX, NZ, SOURCES, LOCAL, CAP)
+    table = lax.dynamic_index_in_dim(table.reshape(NZ, CAP, NZ, -1), z, 2, keepdims=False)
+    table = pick(table.reshape(NZ, -1), (z + jnp.arange(NZ, dtype=jnp.int32)) % NZ ^ z).reshape(1, -1)
+    every = [table]
+    for step in range(1, NX):
+        every.append(shift(table, "x", step))
+    table = jnp.concatenate(every, 0)
+    table = pick(table, (x - jnp.arange(NX, dtype=jnp.int32)) % NX)
+    return table.reshape(NX, NZ, CAP, SOURCES, LOCAL)
 
 
 def gather_up(own):
@@ -336,8 +348,15 @@
     )(x.reshape(1), jnp.asarray(front_table()), strip)
     blocks = gather_up(own)
 
-    codes = exchange_codes(slot_codes(owners[0], live[0], place[0]), z, x)
-    codes = codes.transpose(3, 2, 0, 1, 4)
+    codes = call(
+        codes_kernel,
+        [VMEM] * 3,
+        jax.ShapeDtypeStruct((1, NZ * SOURCES * LOCAL * CAP), jnp.int32),
+        flops=1 << 20,
+        moved=1 << 12,
+    )(owners, live, place)
+    codes = exchange_codes(codes, z, x)
+    codes = codes.transpose(4, 3, 0, 1, 2)
     dead = codes < 0
     rows = jnp.where(dead, WIN, codes // TILES).reshape(LOCAL, PEERS * SLOTS)
     taken = jnp.minimum(rows, WIN - 1)
@@ -377,7 +396,8 @@
             flops=8 * 2 * SUB * SUB * SUB * 2,
             moved=10 << 20,
         )(spots[part], left, right, screen_first, screen_second, got)
-        returned.append(lax.all_to_all(done, plane, split_axis=0, concat_axis=0, tiled=True))
+        done = lax.all_to_all(done, plane, split_axis=0, concat_axis=0, tiled=True)
+        returned.append(done)
     acc = [jax.ShapeDtypeStruct((WIN + 1, QUARTER, LANES), F32)] * NZ
     partial = call(
         sum_first_kernel, [SMEM, VMEM], acc, flops=1 << 28, moved=6 << 20

time: 245 us -> 245 us (level)
  waiting for transfers between devices: 126 us -> 131 us
  starting transfers between devices: 67.1 us -> 64.1 us
    ppermute x5 -> x3, starting transfers between devices: 14.7 us -> 7.85 us  [flip(): return lax.ppermute(value, axis, [(i, i ^ bit) for i in range(size)])]
    ppermute x5 -> x3, waiting for transfers between devices: 7.08 us -> 11.6 us  [flip(): return lax.ppermute(value, axis, [(i, i ^ bit) for i in range(size)])]
    ppermute x19 -> x22, starting transfers between devices: 32.3 us -> 34.8 us  [shift(): lax.ppermute(value, axis, [(i, (i + by) % size) for i in range(size)])]
    unnamed x20 -> x21, local copies, waits for them, and re-layouts: 6.23 us -> 6.98 us
    ppermute x19 -> x22, waiting for transfers between devices: 38.4 us -> 38.8 us  [shift(): lax.ppermute(value, axis, [(i, (i + by) % size) for i in range(size)])]
  transfers between devices with their start and end apart: 28 -> 29, of which waited for: 22 -> 24; matrix products, arithmetic and copies ran while one was open for 3% -> 3% of each run, Pallas kernels for 12% -> 11%
where the time goes in v2:
time: 245 us; the launch traced here: 243 us
  waiting for transfers between devices  131 us (53%)
  starting transfers between devices  64.1 us (26%)
  Pallas kernels  35.8 us (15%)
  local copies, waits for them, and re-layouts  10.9 us (4%)
    all_to_all x2, waiting for transfers between devices, work(): got = lax.all_to_all(sent, plane, split_axis=0, concat_axis=0, tiled=True)  41.2 us
    all_to_all x2, waiting for transfers between devices, work(): done = lax.all_to_all(done, plane, split_axis=0, concat_axis=0, tiled=True)  39 us
    ppermute x22, waiting for transfers between devices, shift(): lax.ppermute(value, axis, [(i, (i + by) % size) for i in range(size)])  38.8 us
    ppermute x22, starting transfers between devices, shift(): lax.ppermute(value, axis, [(i, (i + by) % size) for i in range(size)])  34.8 us
    pallas_call x2, Pallas kernels, work(): call(subgrid_kernel, [SMEM] + [VMEM] * 5, jax.ShapeDtypeStruct((PEERS, SL...  22.4 us
    all_to_all x2, starting transfers between devices, work(): got = lax.all_to_all(sent, plane, split_axis=0, concat_axis=0, tiled=True)  11.9 us
    ppermute x3, waiting for transfers between devices, flip(): return lax.ppermute(value, axis, [(i, i ^ bit) for i in range(size)])  11.6 us
    all_to_all x2, starting transfers between devices, work(): done = lax.all_to_all(done, plane, split_axis=0, concat_axis=0, tiled=True)  9.57 us
  transfers between devices with their start and end apart: 29, of which 24 were waited for; matrix products, arithmetic and copies ran while one was open for 3% of the time, Pallas kernels for 11%

profile of v2, /device:TPU:32, one launch (start us, length us, event | category | flops | bytes accessed | tf_op | source)
XLA Modules:
  0.0 242.9 jit_solution(13217666400530015255)
XLA Ops:
  7.1 4.0 %collective-permute-start = (s32[1,256]{1,0:T(1,128)S(1)}, s32[1,256]{1,0:T(1,128)S(1)}, u32[]{:S(2)}, u32[]{:S(2)}) collective-permute-start(s32[1,256]{1,0:T(1,128)S(1)} %shard_map.100), channel_id=1, source_target_pairs={{0,32},{32,0},{64,96},{96,64},{128,160},{160,128},{192,224},{224,1... | collective-permute-start | bytes 3080 | tf_op jit(solution)/shard_map/ppermute | solution.py:297
  11.1 3.4 %collective-permute-done = s32[1,256]{1,0:T(1,128)S(1)} collective-permute-done((s32[1,256]{1,0:T(1,128)S(1)}, s32[1,256]{1,0:T(1,128)S(1)}, u32[]{:S(2)}, u32[]{:S(2)}) %collective-permute-start) | collective-permute-done | bytes 1056 | tf_op jit(solution)/shard_map/ppermute | solution.py:297
  15.3 3.7 %collective-permute-done.1 = s32[2,256]{1,0:T(2,128)S(1)} collective-permute-done((s32[2,256]{1,0:T(2,128)S(1)}, s32[2,256]{1,0:T(2,128)S(1)}, u32[]{:S(2)}, u32[]{:S(2)}) %collective-permute-start.1) | collective-permute-done | bytes 2080 | tf_op jit(solution)/shard_map/ppermute | solution.py:297
  22.2 4.4 %collective-permute-done.2 = s32[4,256]{1,0:T(4,128)S(1)} collective-permute-done((s32[4,256]{1,0:T(4,128)S(1)}, s32[4,256]{1,0:T(4,128)S(1)}, u32[]{:S(2)}, u32[]{:S(2)}) %collective-permute-start.2) | collective-permute-done | bytes 4128 | tf_op jit(solution)/shard_map/ppermute | solution.py:297
  35.4 5.2 %collective-permute-done.7.refs_2_ = bf16[64,16,128]{2,1,0:T(8,128)(2,1)S(1)} collective-permute-done((bf16[64,16,128]{2,1,0:T(8,128)(2,1)S(1)}, bf16[64,16,128]{2,1,0:T(8,128)(2,1)S(1)}, u32[]{:S(2)}, u32[]{:S(2)}) %collective-permute-start.7) | collective-permute-done | bytes 262176 | tf_op jit(solution)/shard_map/ppermute | solution.py:287
  43.4 6.9 %collective-permute-done.11.refs_4_ = bf16[64,16,128]{2,1,0:T(8,128)(2,1)S(1)} collective-permute-done((bf16[64,16,128]{2,1,0:T(8,128)(2,1)S(1)}, bf16[64,16,128]{2,1,0:T(8,128)(2,1)S(1)}, u32[]{:S(2)}, u32[]{:S(2)}) %collective-permute-start.11) | collective-permute-done | bytes 262176 | tf_op jit(solution)/shard_map/ppermute | solution.py:287
  58.8 6.9 %all-to-all-start = ((bf16[32,17,16,128]{3,2,1,0:T(8,128)(2,1)}), bf16[32,17,16,128]{3,2,1,0:T(8,128)(2,1)}, u32[]{:S(2)}, u32[]{:S(2)}) async-start(bf16[32,17,16,128]{3,2,1,0:T(8,128)(2,1)} %shard_map.102), calls=%async_computation | async-start | bytes 4456448 | tf_op jit(solution)/shard_map/all_to_all | solution.py:380
  68.8 25.7 %all-to-all-done.slabs_ref = bf16[32,17,16,128]{3,2,1,0:T(8,128)(2,1)} async-done(((bf16[32,17,16,128]{3,2,1,0:T(8,128)(2,1)}), bf16[32,17,16,128]{3,2,1,0:T(8,128)(2,1)}, u32[]{:S(2)}, u32[]{:S(2)}) %all-to-all-start) | async-done | bytes 2228256 | tf_op jit(solution)/shard_map/all_to_all | solution.py:380
  94.5 4.9 %all-to-all-start.1 = ((bf16[32,16,16,128]{3,2,1,0:T(8,128)(2,1)}), bf16[32,16,16,128]{3,2,1,0:T(8,128)(2,1)}, u32[]{:S(2)}, u32[]{:S(2)}) async-start(bf16[32,16,16,128]{3,2,1,0:T(8,128)(2,1)} %shard_map.103), calls=%async_computation.1 | async-start | bytes 4194304 | tf_op jit(solution)/shard_map/all_to_all | solution.py:380
  100.3 11.2 %shard_map.105 = bf16[32,16,16,128]{3,2,1,0:T(8,128)(2,1)} custom-call(s32[128]{0:T(128)S(1)} %squeeze.26.tags_ref, bf16[512,1024]{1,0:T(8,128)(2,1)S(1)} %copy-done.7, bf16[1024,1024]{1,0:T(8,128)(2,1)} %constant.123.clone.right_ref, bf16[2,512,512]{2,1,0:T(8,128)(2,1)S(1)} %copy-done.5, bf16[2,512,512]{2,1,0:T(8,128)(2,1)S(1)} %copy-done.6, ...), custom_call_target="tpu_custom_call" | custom-call | flops 4294967296 | bytes 10485760 | tf_op jit(solution)/shard_map/pallas_call | solution.py:386
  111.6 15.5 %all-to-all-done.1.slabs_ref = bf16[32,16,16,128]{3,2,1,0:T(8,128)(2,1)} async-done(((bf16[32,16,16,128]{3,2,1,0:T(8,128)(2,1)}), bf16[32,16,16,128]{3,2,1,0:T(8,128)(2,1)}, u32[]{:S(2)}, u32[]{:S(2)}) %all-to-all-start.1) | async-done | bytes 2097184 | tf_op jit(solution)/shard_map/all_to_all | solution.py:380
  127.1 4.8 %all-to-all-start.3 = ((bf16[32,16,16,128]{3,2,1,0:T(8,128)(2,1)}), bf16[32,16,16,128]{3,2,1,0:T(8,128)(2,1)}, u32[]{:S(2)}, u32[]{:S(2)}) async-start(bf16[32,16,16,128]{3,2,1,0:T(8,128)(2,1)} %shard_map.105), calls=%async_computation.3 | async-start | bytes 4194304 | tf_op jit(solution)/shard_map/all_to_all | solution.py:399
  131.9 11.2 %shard_map.104 = bf16[32,16,16,128]{3,2,1,0:T(8,128)(2,1)} custom-call(s32[128]{0:T(128)S(1)} %squeeze.23.tags_ref, bf16[512,1024]{1,0:T(8,128)(2,1)S(1)} %copy-done.7, bf16[1024,1024]{1,0:T(8,128)(2,1)} %constant.123.clone.right_ref, bf16[2,512,512]{2,1,0:T(8,128)(2,1)S(1)} %copy-done.5, bf16[2,512,512]{2,1,0:T(8,128)(2,1)S(1)} %copy-done.6, ...), custom_call_target="tpu_custom_call" | custom-call | flops 4294967296 | bytes 10485760 | tf_op jit(solution)/shard_map/pallas_call | solution.py:386
  143.1 16.4 %all-to-all-done.3.slots_ref = bf16[32,16,16,128]{3,2,1,0:T(8,128)(2,1)} async-done(((bf16[32,16,16,128]{3,2,1,0:T(8,128)(2,1)}), bf16[32,16,16,128]{3,2,1,0:T(8,128)(2,1)}, u32[]{:S(2)}, u32[]{:S(2)}) %all-to-all-start.3) | async-done | bytes 2097184 | tf_op jit(solution)/shard_map/all_to_all | solution.py:399
  159.5 4.8 %all-to-all-start.2 = ((bf16[32,16,16,128]{3,2,1,0:T(8,128)(2,1)}), bf16[32,16,16,128]{3,2,1,0:T(8,128)(2,1)}, u32[]{:S(2)}, u32[]{:S(2)}) async-start(bf16[32,16,16,128]{3,2,1,0:T(8,128)(2,1)} %shard_map.104), calls=%async_computation.2 | async-start | bytes 4194304 | tf_op jit(solution)/shard_map/all_to_all | solution.py:399
  169.4 22.6 %all-to-all-done.2.slots_ref = bf16[32,16,16,128]{3,2,1,0:T(8,128)(2,1)} async-done(((bf16[32,16,16,128]{3,2,1,0:T(8,128)(2,1)}), bf16[32,16,16,128]{3,2,1,0:T(8,128)(2,1)}, u32[]{:S(2)}, u32[]{:S(2)}) %all-to-all-start.2) | async-done | bytes 2097184 | tf_op jit(solution)/shard_map/all_to_all | solution.py:399
  196.0 3.5 %collective-permute-start.18 = (bf16[32,16,128]{2,1,0:T(8,128)(2,1)S(1)}, bf16[32,16,128]{2,1,0:T(8,128)(2,1)S(1)}, u32[]{:S(2)}, u32[]{:S(2)}) collective-permute-start(bf16[32,16,128]{2,1,0:T(8,128)(2,1)S(1)} %get-tuple-element.46), channel_id=1, source_target_pairs={{0,224},{32,0},{64,32},{96,64},{128,96},{160,128},{192,160},{224,1... | collective-permute-start | bytes 393224 | tf_op jit(solution)/shard_map/ppermute | solution.py:287
  202.2 3.4 %collective-permute-start.19 = (bf16[64,16,128]{2,1,0:T(8,128)(2,1)S(1)}, bf16[64,16,128]{2,1,0:T(8,128)(2,1)S(1)}, u32[]{:S(2)}, u32[]{:S(2)}) collective-permute-start(bf16[64,16,128]{2,1,0:T(8,128)(2,1)S(1)} %pad_maximum_fusion.1), channel_id=1, source_target_pairs={{0,224},{32,0},{64,32},{96,64},{128,96},{160,128},{192,160},{224,1... | collective-permute-start | bytes 786440 | tf_op jit(solution)/shard_map/ppermute | solution.py:287
  206.1 3.7 %collective-permute-done.19 = bf16[64,16,128]{2,1,0:T(8,128)(2,1)S(1)} collective-permute-done((bf16[64,16,128]{2,1,0:T(8,128)(2,1)S(1)}, bf16[64,16,128]{2,1,0:T(8,128)(2,1)S(1)}, u32[]{:S(2)}, u32[]{:S(2)}) %collective-permute-start.19) | collective-permute-done | bytes 262176 | tf_op jit(solution)/shard_map/ppermute | solution.py:287
  209.9 3.4 %collective-permute-start.20 = (bf16[64,16,128]{2,1,0:T(8,128)(2,1)S(1)}, bf16[64,16,128]{2,1,0:T(8,128)(2,1)S(1)}, u32[]{:S(2)}, u32[]{:S(2)}) collective-permute-start(bf16[64,16,128]{2,1,0:T(8,128)(2,1)S(1)} %add_convert_fusion.2), channel_id=1, source_target_pairs={{0,224},{32,0},{64,32},{96,64},{128,96},{160,128},{192,160},{224,1... | collective-permute-start | bytes 786440 | tf_op jit(solution)/shard_map/ppermute | solution.py:287
  213.9 3.3 %collective-permute-done.20 = bf16[64,16,128]{2,1,0:T(8,128)(2,1)S(1)} collective-permute-done((bf16[64,16,128]{2,1,0:T(8,128)(2,1)S(1)}, bf16[64,16,128]{2,1,0:T(8,128)(2,1)S(1)}, u32[]{:S(2)}, u32[]{:S(2)}) %collective-permute-start.20) | collective-permute-done | bytes 262176 | tf_op jit(solution)/shard_map/ppermute | solution.py:287
  217.3 3.8 %collective-permute-start.21 = (bf16[64,16,128]{2,1,0:T(8,128)(2,1)S(1)}, bf16[64,16,128]{2,1,0:T(8,128)(2,1)S(1)}, u32[]{:S(2)}, u32[]{:S(2)}) collective-permute-start(bf16[64,16,128]{2,1,0:T(8,128)(2,1)S(1)} %add_convert_fusion.1), channel_id=1, source_target_pairs={{0,224},{32,0},{64,32},{96,64},{128,96},{160,128},{192,160},{224,1... | collective-permute-start | bytes 786440 | tf_op jit(solution)/shard_map/ppermute | solution.py:287
  224.9 4.5 %collective-permute-done.17 = bf16[64,16,128]{2,1,0:T(8,128)(2,1)S(1)} collective-permute-done((bf16[64,16,128]{2,1,0:T(8,128)(2,1)S(1)}, bf16[64,16,128]{2,1,0:T(8,128)(2,1)S(1)}, u32[]{:S(2)}, u32[]{:S(2)}) %collective-permute-start.17) | collective-permute-done | bytes 262176 | tf_op jit(solution)/shard_map/ppermute | solution.py:287
  231.6 5.0 %collective-permute-start.23 = (bf16[16,16,128]{2,1,0:T(8,128)(2,1)S(1)}, bf16[16,16,128]{2,1,0:T(8,128)(2,1)S(1)}, u32[]{:S(2)}, u32[]{:S(2)}) collective-permute-start(bf16[16,16,128]{2,1,0:T(8,128)(2,1)S(1)} %get-tuple-element.42), channel_id=1, source_target_pairs={{0,2},{1,3},{2,0},{3,1},{4,6},{5,7},{6,4},{7,5},{8,10},{9,11},{10,... | collective-permute-start | bytes 196616 | tf_op jit(solution)/shard_map/ppermute | solution.py:287
  (115 shorter events, 60.1 us)
Async XLA Ops:
  2.4 29.1 %collective-permute-start.6 = (bf16[64,16,128]{2,1,0:T(8,128)(2,1)S(1)}, bf16[64,16,128]{2,1,0:T(8,128)(2,1)S(1)}, u32[]{:S(2)}, u32[]{:S(2)}) collective-permute-start(bf16[64,16,128]{2,1,0:T(8,128)(2,1)S(1)} %shard_map.101.refs_0_), channel_id=1, source_target_pairs={{0,224},{32,0},{64,32},{96,64},{128,96},{160,128},{192,160},{224,1... | collective-permute-start | bytes 786440 | tf_op jit(solution)/shard_map/ppermute | solution.py:287
  4.3 27.3 %collective-permute-start.9 = (bf16[64,16,128]{2,1,0:T(8,128)(2,1)S(1)}, bf16[64,16,128]{2,1,0:T(8,128)(2,1)S(1)}, u32[]{:S(2)}, u32[]{:S(2)}) collective-permute-start(bf16[64,16,128]{2,1,0:T(8,128)(2,1)S(1)} %shard_map.101.refs_0_), channel_id=1, source_target_pairs={{0,32},{32,64},{64,96},{96,128},{128,160},{160,192},{192,224},{224... | collective-permute-start | bytes 786440 | tf_op jit(solution)/shard_map/ppermute | solution.py:287
  7.1 7.5 %collective-permute-start = (s32[1,256]{1,0:T(1,128)S(1)}, s32[1,256]{1,0:T(1,128)S(1)}, u32[]{:S(2)}, u32[]{:S(2)}) collective-permute-start(s32[1,256]{1,0:T(1,128)S(1)} %shard_map.100), channel_id=1, source_target_pairs={{0,32},{32,0},{64,96},{96,64},{128,160},{160,128},{192,224},{224,1... | collective-permute-start | bytes 3080 | tf_op jit(solution)/shard_map/ppermute | solution.py:297
  19.1 7.6 %collective-permute-start.2 = (s32[4,256]{1,0:T(4,128)S(1)}, s32[4,256]{1,0:T(4,128)S(1)}, u32[]{:S(2)}, u32[]{:S(2)}) collective-permute-start(s32[4,256]{1,0:T(4,128)S(1)} %pad_add_fusion.1), channel_id=1, source_target_pairs={{0,128},{32,160},{64,192},{96,224},{128,0},{160,32},{192,64},{224,... | collective-permute-start | bytes 12296 | tf_op jit(solution)/shard_map/ppermute | solution.py:297
  27.1 6.6 %collective-permute-start.5 = (s32[1,256]{1,0:T(1,128)S(1)}, s32[1,256]{1,0:T(1,128)S(1)}, u32[]{:S(2)}, u32[]{:S(2)}) collective-permute-start(s32[1,256]{1,0:T(1,128)S(1)} %reshape.128), channel_id=1, source_target_pairs={{0,3},{1,0},{2,1},{3,2},{4,7},{5,4},{6,5},{7,6},{8,11},{9,8},{10,9... | collective-permute-start | bytes 3080 | tf_op jit(solution)/shard_map/ppermute | solution.py:287
  31.5 9.1 %collective-permute-start.7 = (bf16[64,16,128]{2,1,0:T(8,128)(2,1)S(1)}, bf16[64,16,128]{2,1,0:T(8,128)(2,1)S(1)}, u32[]{:S(2)}, u32[]{:S(2)}) collective-permute-start(bf16[64,16,128]{2,1,0:T(8,128)(2,1)S(1)} %collective-permute-done.6.refs_1_), channel_id=1, source_target_pairs={{0,224},{32,0},{64,32},{96,64},{128,96},{160,128},{192,160},{224,1... | collective-permute-start | bytes 786440 | tf_op jit(solution)/shard_map/ppermute | solution.py:287
  31.7 9.6 %collective-permute-start.10 = (bf16[64,16,128]{2,1,0:T(8,128)(2,1)S(1)}, bf16[64,16,128]{2,1,0:T(8,128)(2,1)S(1)}, u32[]{:S(2)}, u32[]{:S(2)}) collective-permute-start(bf16[64,16,128]{2,1,0:T(8,128)(2,1)S(1)} %collective-permute-done.9.refs_6_), channel_id=1, source_target_pairs={{0,32},{32,64},{64,96},{96,128},{128,160},{160,192},{192,224},{224... | collective-permute-start | bytes 786440 | tf_op jit(solution)/shard_map/ppermute | solution.py:287
  40.6 9.7 %collective-permute-start.8 = (bf16[64,16,128]{2,1,0:T(8,128)(2,1)S(1)}, bf16[64,16,128]{2,1,0:T(8,128)(2,1)S(1)}, u32[]{:S(2)}, u32[]{:S(2)}) collective-permute-start(bf16[64,16,128]{2,1,0:T(8,128)(2,1)S(1)} %collective-permute-done.7.refs_2_), channel_id=1, source_target_pairs={{0,224},{32,0},{64,32},{96,64},{128,96},{160,128},{192,160},{224,1... | collective-permute-start | bytes 786440 | tf_op jit(solution)/shard_map/ppermute | solution.py:287
  41.3 9.0 %collective-permute-start.11 = (bf16[64,16,128]{2,1,0:T(8,128)(2,1)S(1)}, bf16[64,16,128]{2,1,0:T(8,128)(2,1)S(1)}, u32[]{:S(2)}, u32[]{:S(2)}) collective-permute-start(bf16[64,16,128]{2,1,0:T(8,128)(2,1)S(1)} %collective-permute-done.10.refs_5_), channel_id=1, source_target_pairs={{0,32},{32,64},{64,96},{96,128},{128,160},{160,192},{192,224},{224... | collective-permute-start | bytes 786440 | tf_op jit(solution)/shard_map/ppermute | solution.py:287
  50.3 6.0 %collective-permute-start.12 = (bf16[32,16,128]{2,1,0:T(8,128)(2,1)S(1)}, bf16[32,16,128]{2,1,0:T(8,128)(2,1)S(1)}, u32[]{:S(2)}, u32[]{:S(2)}) collective-permute-start(bf16[32,16,128]{2,1,0:T(8,128)(2,1)S(1)} %slice.68), channel_id=1, source_target_pairs={{0,32},{32,64},{64,96},{96,128},{128,160},{160,192},{192,224},{224... | collective-permute-start | bytes 393224 | tf_op jit(solution)/shard_map/ppermute | solution.py:287
  58.8 35.7 %all-to-all-start = ((bf16[32,17,16,128]{3,2,1,0:T(8,128)(2,1)}), bf16[32,17,16,128]{3,2,1,0:T(8,128)(2,1)}, u32[]{:S(2)}, u32[]{:S(2)}) async-start(bf16[32,17,16,128]{3,2,1,0:T(8,128)(2,1)} %shard_map.102), calls=%async_computation | async-start | bytes 4456448 | tf_op jit(solution)/shard_map/all_to_all | solution.py:380
  94.5 32.6 %all-to-all-start.1 = ((bf16[32,16,16,128]{3,2,1,0:T(8,128)(2,1)}), bf16[32,16,16,128]{3,2,1,0:T(8,128)(2,1)}, u32[]{:S(2)}, u32[]{:S(2)}) async-start(bf16[32,16,16,128]{3,2,1,0:T(8,128)(2,1)} %shard_map.103), calls=%async_computation.1 | async-start | bytes 4194304 | tf_op jit(solution)/shard_map/all_to_all | solution.py:380
  127.1 32.5 %all-to-all-start.3 = ((bf16[32,16,16,128]{3,2,1,0:T(8,128)(2,1)}), bf16[32,16,16,128]{3,2,1,0:T(8,128)(2,1)}, u32[]{:S(2)}, u32[]{:S(2)}) async-start(bf16[32,16,16,128]{3,2,1,0:T(8,128)(2,1)} %shard_map.105), calls=%async_computation.3 | async-start | bytes 4194304 | tf_op jit(solution)/shard_map/all_to_all | solution.py:399
  159.5 32.5 %all-to-all-start.2 = ((bf16[32,16,16,128]{3,2,1,0:T(8,128)(2,1)}), bf16[32,16,16,128]{3,2,1,0:T(8,128)(2,1)}, u32[]{:S(2)}, u32[]{:S(2)}) async-start(bf16[32,16,16,128]{3,2,1,0:T(8,128)(2,1)} %shard_map.104), calls=%async_computation.2 | async-start | bytes 4194304 | tf_op jit(solution)/shard_map/all_to_all | solution.py:399
  196.0 6.1 %collective-permute-start.18 = (bf16[32,16,128]{2,1,0:T(8,128)(2,1)S(1)}, bf16[32,16,128]{2,1,0:T(8,128)(2,1)S(1)}, u32[]{:S(2)}, u32[]{:S(2)}) collective-permute-start(bf16[32,16,128]{2,1,0:T(8,128)(2,1)S(1)} %get-tuple-element.46), channel_id=1, source_target_pairs={{0,224},{32,0},{64,32},{96,64},{128,96},{160,128},{192,160},{224,1... | collective-permute-start | bytes 393224 | tf_op jit(solution)/shard_map/ppermute | solution.py:287
  199.6 6.3 %collective-permute-start.14 = (bf16[32,16,128]{2,1,0:T(8,128)(2,1)S(1)}, bf16[32,16,128]{2,1,0:T(8,128)(2,1)S(1)}, u32[]{:S(2)}, u32[]{:S(2)}) collective-permute-start(bf16[32,16,128]{2,1,0:T(8,128)(2,1)S(1)} %get-tuple-element.45), channel_id=1, source_target_pairs={{0,32},{32,64},{64,96},{96,128},{128,160},{160,192},{192,224},{224... | collective-permute-start | bytes 393224 | tf_op jit(solution)/shard_map/ppermute | solution.py:287
  202.2 7.6 %collective-permute-start.19 = (bf16[64,16,128]{2,1,0:T(8,128)(2,1)S(1)}, bf16[64,16,128]{2,1,0:T(8,128)(2,1)S(1)}, u32[]{:S(2)}, u32[]{:S(2)}) collective-permute-start(bf16[64,16,128]{2,1,0:T(8,128)(2,1)S(1)} %pad_maximum_fusion.1), channel_id=1, source_target_pairs={{0,224},{32,0},{64,32},{96,64},{128,96},{160,128},{192,160},{224,1... | collective-permute-start | bytes 786440 | tf_op jit(solution)/shard_map/ppermute | solution.py:287
  206.0 7.7 %collective-permute-start.15 = (bf16[64,16,128]{2,1,0:T(8,128)(2,1)S(1)}, bf16[64,16,128]{2,1,0:T(8,128)(2,1)S(1)}, u32[]{:S(2)}, u32[]{:S(2)}) collective-permute-start(bf16[64,16,128]{2,1,0:T(8,128)(2,1)S(1)} %pad_maximum_fusion), channel_id=1, source_target_pairs={{0,32},{32,64},{64,96},{96,128},{128,160},{160,192},{192,224},{224... | collective-permute-start | bytes 786440 | tf_op jit(solution)/shard_map/ppermute | solution.py:287
  209.9 7.3 %collective-permute-start.20 = (bf16[64,16,128]{2,1,0:T(8,128)(2,1)S(1)}, bf16[64,16,128]{2,1,0:T(8,128)(2,1)S(1)}, u32[]{:S(2)}, u32[]{:S(2)}) collective-permute-start(bf16[64,16,128]{2,1,0:T(8,128)(2,1)S(1)} %add_convert_fusion.2), channel_id=1, source_target_pairs={{0,224},{32,0},{64,32},{96,64},{128,96},{160,128},{192,160},{224,1... | collective-permute-start | bytes 786440 | tf_op jit(solution)/shard_map/ppermute | solution.py:287
  213.8 7.7 %collective-permute-start.16 = (bf16[64,16,128]{2,1,0:T(8,128)(2,1)S(1)}, bf16[64,16,128]{2,1,0:T(8,128)(2,1)S(1)}, u32[]{:S(2)}, u32[]{:S(2)}) collective-permute-start(bf16[64,16,128]{2,1,0:T(8,128)(2,1)S(1)} %add_convert_fusion.4), channel_id=1, source_target_pairs={{0,32},{32,64},{64,96},{96,128},{128,160},{160,192},{192,224},{224... | collective-permute-start | bytes 786440 | tf_op jit(solution)/shard_map/ppermute | solution.py:287
  217.3 7.7 %collective-permute-start.21 = (bf16[64,16,128]{2,1,0:T(8,128)(2,1)S(1)}, bf16[64,16,128]{2,1,0:T(8,128)(2,1)S(1)}, u32[]{:S(2)}, u32[]{:S(2)}) collective-permute-start(bf16[64,16,128]{2,1,0:T(8,128)(2,1)S(1)} %add_convert_fusion.1), channel_id=1, source_target_pairs={{0,224},{32,0},{64,32},{96,64},{128,96},{160,128},{192,160},{224,1... | collective-permute-start | bytes 786440 | tf_op jit(solution)/shard_map/ppermute | solution.py:287
  221.6 7.8 %collective-permute-start.17 = (bf16[64,16,128]{2,1,0:T(8,128)(2,1)S(1)}, bf16[64,16,128]{2,1,0:T(8,128)(2,1)S(1)}, u32[]{:S(2)}, u32[]{:S(2)}) collective-permute-start(bf16[64,16,128]{2,1,0:T(8,128)(2,1)S(1)} %add_convert_fusion.3), channel_id=1, source_target_pairs={{0,32},{32,64},{64,96},{96,128},{128,160},{160,192},{192,224},{224... | collective-permute-start | bytes 786440 | tf_op jit(solution)/shard_map/ppermute | solution.py:287
  229.5 7.9 %collective-permute-start.22 = (bf16[16,16,128]{2,1,0:T(8,128)(2,1)S(1)}, bf16[16,16,128]{2,1,0:T(8,128)(2,1)S(1)}, u32[]{:S(2)}, u32[]{:S(2)}) collective-permute-start(bf16[16,16,128]{2,1,0:T(8,128)(2,1)S(1)} %get-tuple-element.43), channel_id=1, source_target_pairs={{0,1},{1,2},{2,3},{3,0},{4,5},{5,6},{6,7},{7,4},{8,9},{9,10},{10,1... | collective-permute-start | bytes 196616 | tf_op jit(solution)/shard_map/ppermute | solution.py:287
  231.6 8.0 %collective-permute-start.23 = (bf16[16,16,128]{2,1,0:T(8,128)(2,1)S(1)}, bf16[16,16,128]{2,1,0:T(8,128)(2,1)S(1)}, u32[]{:S(2)}, u32[]{:S(2)}) collective-permute-start(bf16[16,16,128]{2,1,0:T(8,128)(2,1)S(1)} %get-tuple-element.42), channel_id=1, source_target_pairs={{0,2},{1,3},{2,0},{3,1},{4,6},{5,7},{6,4},{7,5},{8,10},{9,11},{10,... | collective-permute-start | bytes 196616 | tf_op jit(solution)/shard_map/ppermute | solution.py:287
  (14 other events, 154.9 us)

commit v3 on v2

--- a/solution.py
+++ b/solution.py
@@ -59,7 +59,12 @@
 
 def last_table():
     real, imag = dft(WIN)
-    return np.concatenate([real, -imag], 0).astype(np.float32)
+    rest = np.concatenate([real, -imag], 0).astype(np.float32)
+    terms = []
+    for _ in range(3):
+        terms.append(rest.astype(BF))
+        rest = rest - terms[-1].astype(np.float32)
+    return np.concatenate(terms, 1)
 
 
 def swap_halves(x):
@@ -70,7 +75,8 @@
     return lax.broadcasted_iota(jnp.int32, shape, len(shape) - 1) < WIN
 
 
-def front_kernel(where_ref, table_ref, strip_ref, out_ref):
+def front_kernel(where_ref, table_ref, strip_ref, owner_ref, live_ref, place_ref, out_ref, codes_ref):
+    codes_kernel(owner_ref, live_ref, place_ref, codes_ref)
     table = table_ref[where_ref[0]]
     for j in range(WIN // 2):
         cols = pl.ds(j * LANES, LANES)
@@ -83,27 +89,38 @@
 
 
 def codes_kernel(owner_ref, live_ref, place_ref, out_ref):
-    shape = (WIN, NZ * SOURCES * LOCAL)
-    window = lax.broadcasted_iota(jnp.int32, shape, 0)
-    subgrid = lax.broadcasted_iota(jnp.int32, shape, 1)
+    shape = (NZ * SOURCES * LOCAL, WIN)
+    subgrid = lax.broadcasted_iota(jnp.int32, shape, 0)
+    window = lax.broadcasted_iota(jnp.int32, shape, 1)
     count = jnp.zeros(shape, F32)
-    value = jnp.zeros(shape, F32)
+    which = jnp.zeros(shape, jnp.int32)
+    tile = jnp.zeros(shape, jnp.int32)
     for k in range(3):
-        entry = (0, slice(None), slice(k, k + 1))
-        hit = owner_ref[entry] == subgrid
-        code = (window * TILES + place_ref[entry] + 1).astype(F32)
+        hit = owner_ref[k] == subgrid
+        used = hit & (live_ref[k] == 1)
         count += jnp.where(hit, 1.0, 0.0)
-        value += jnp.where(hit & (live_ref[entry] == 1), code, 0.0)
+        which += jnp.where(used, window + 1, 0)
+        tile += jnp.where(used, place_ref[k], 0)
     square = (WIN, WIN)
-    earlier = lax.broadcasted_iota(jnp.int32, square, 1) < lax.broadcasted_iota(
-        jnp.int32, square, 0
+    earlier = lax.broadcasted_iota(jnp.int32, square, 0) < lax.broadcasted_iota(
+        jnp.int32, square, 1
     )
     rank = jnp.dot(
-        jnp.where(earlier, 1.0, 0.0).astype(BF), count.astype(BF), preferred_element_type=F32
-    )
+        count.astype(BF), jnp.where(earlier, 1.0, 0.0).astype(BF), preferred_element_type=F32
+    )
+    ones = jnp.ones((8, WIN), BF)
+
+    def as_row(value):
+        return lax.dot_general(
+            ones, value.astype(F32).astype(BF), (((1,), (1,)), ((), ())),
+            preferred_element_type=F32,
+        )[:1].astype(jnp.int32)
+
     for cap in range(CAP):
-        mine = jnp.sum(jnp.where(rank == float(cap), value, 0.0), axis=0, keepdims=True)
-        out_ref[:, cap * shape[1] : (cap + 1) * shape[1]] = mine.astype(jnp.int32) - 1
+        mine = rank == float(cap)
+        number = as_row(jnp.where(mine, which, 0))
+        code = (number - 1) * TILES + as_row(jnp.where(mine, tile, 0))
+        out_ref[:, cap * shape[0] : (cap + 1) * shape[0]] = jnp.where(number > 0, code, -1)
 
 
 def pack_kernel(extra, rows_ref, *refs):
@@ -246,14 +263,14 @@
         q = (where_ref[0] + NX - s) % NX
         rows = pl.ds(pl.multiple_of(q * QUARTER, QUARTER), QUARTER)
         for w in range(count):
-            tile_ref[w, rows, :] = blocks[s][w].astype(F32)
+            tile_ref[w, rows, :] = blocks[s][w]
     for j in range(count // 2):
         ends = []
         for h in range(2):
+            tile = tile_ref[2 * j + h]
             both = jnp.dot(
                 table_ref[...],
-                tile_ref[2 * j + h],
-                precision=lax.Precision.HIGHEST,
+                jnp.concatenate([tile] * 3, 0),
                 preferred_element_type=F32,
             )
             turned = swap_halves(both[WIN:])
@@ -267,9 +284,10 @@
 
 VMEM = pl.BlockSpec(memory_space=pltpu.VMEM)
 SMEM = pl.BlockSpec(memory_space=pltpu.SMEM)
-
-
-def call(kernel, specs, out, scratch=(), flops=0, moved=0):
+FRONT_LIMIT = (64 << 20) - (256 << 10)
+
+
+def call(kernel, specs, out, scratch=(), flops=0, moved=0, limit=48 << 20):
     outs = jax.tree.map(lambda _: VMEM, out)
     return pl.pallas_call(
         kernel,
@@ -278,7 +296,7 @@
         out_shape=out,
         scratch_shapes=list(scratch),
         cost_estimate=pl.CostEstimate(flops=flops, bytes_accessed=moved, transcendentals=0),
-        compiler_params=pltpu.CompilerParams(vmem_limit_bytes=48 << 20),
+        compiler_params=pltpu.CompilerParams(vmem_limit_bytes=limit),
     )
 
 
@@ -343,18 +361,20 @@
     z, x = lax.axis_index("z"), lax.axis_index("x")
     plane = ("y", "k", "x")
     block = jax.ShapeDtypeStruct((WIN, QUARTER, LANES), BF)
-    own = call(
-        front_kernel, [SMEM, VMEM, VMEM], block, flops=2 * 32 * 128 * 4096, moved=2 << 20
-    )(x.reshape(1), jnp.asarray(front_table()), strip)
+    own, codes = call(
+        front_kernel,
+        [SMEM] + [VMEM] * 5,
+        [block, jax.ShapeDtypeStruct((1, NZ * SOURCES * LOCAL * CAP), jnp.int32)],
+        flops=2 * 32 * 128 * 4096,
+        moved=2 << 20,
+        limit=FRONT_LIMIT,
+    )(
+        x.reshape(1),
+        jnp.asarray(front_table()),
+        strip,
+        *(a.transpose(2, 0, 1) for a in (owners, live, place)),
+    )
     blocks = gather_up(own)
-
-    codes = call(
-        codes_kernel,
-        [VMEM] * 3,
-        jax.ShapeDtypeStruct((1, NZ * SOURCES * LOCAL * CAP), jnp.int32),
-        flops=1 << 20,
-        moved=1 << 12,
-    )(owners, live, place)
     codes = exchange_codes(codes, z, x)
     codes = codes.transpose(4, 3, 0, 1, 2)
     dead = codes < 0
@@ -420,7 +440,7 @@
         last_kernel,
         [SMEM] + [VMEM] * (1 + NX),
         jax.ShapeDtypeStruct((2, WIN, count * WIN), F32),
-        scratch=[pltpu.VMEM((count, WIN, LANES), F32)],
+        scratch=[pltpu.VMEM((count, WIN, LANES), BF)],
         flops=1 << 28,
         moved=1 << 20,
     )(x.reshape(1), jnp.asarray(last_table()), *pieces)

time: 245 us -> 246 us (level)
  local copies, waits for them, and re-layouts: 10.9 us -> 6.6 us
    unnamed x21 -> x16, local copies, waits for them, and re-layouts: 6.98 us -> 2.7 us
    ppermute x3, waiting for transfers between devices: 11.6 us -> 15.2 us  [flip(): return lax.ppermute(value, axis, [(i, i ^ bit) for i in range(size)])]
  transfers between devices with their start and end apart: 29 -> 29, of which waited for: 24 -> 23; matrix products, arithmetic and copies ran while one was open for 3% -> 3% of each run, Pallas kernels for 11% -> 11%
where the time goes in v3:
time: 246 us; the launch traced here: 244 us
  waiting for transfers between devices  133 us (54%)
  starting transfers between devices  63.7 us (26%)
  Pallas kernels  37.2 us (15%)
  local copies, waits for them, and re-layouts  6.6 us (3%)
  other arithmetic  2.95 us (1%)
    all_to_all x2, waiting for transfers between devices, work(): got = lax.all_to_all(sent, plane, split_axis=0, concat_axis=0, tiled=True)  41.2 us
    all_to_all x2, waiting for transfers between devices, work(): done = lax.all_to_all(done, plane, split_axis=0, concat_axis=0, tiled=True)  39 us
    ppermute x22, waiting for transfers between devices, shift(): lax.ppermute(value, axis, [(i, (i + by) % size) for i in range(size)])  37.7 us
    ppermute x22, starting transfers between devices, shift(): lax.ppermute(value, axis, [(i, (i + by) % size) for i in range(size)])  35.2 us
    pallas_call x2, Pallas kernels, work(): call(subgrid_kernel, [SMEM] + [VMEM] * 5, jax.ShapeDtypeStruct((PEERS, SL...  22.4 us
    ppermute x3, waiting for transfers between devices, flip(): return lax.ppermute(value, axis, [(i, i ^ bit) for i in range(size)])  15.2 us
    all_to_all x2, starting transfers between devices, work(): got = lax.all_to_all(sent, plane, split_axis=0, concat_axis=0, tiled=True)  11.9 us
    all_to_all x2, starting transfers between devices, work(): done = lax.all_to_all(done, plane, split_axis=0, concat_axis=0, tiled=True)  9.58 us
  transfers between devices with their start and end apart: 29, of which 23 were waited for; matrix products, arithmetic and copies ran while one was open for 3% of the time, Pallas kernels for 11%

profile of v3, /device:TPU:32, one launch (start us, length us, event | category | flops | bytes accessed | tf_op | source)
XLA Modules:
  0.0 243.9 jit_solution(11214655511072480667)
XLA Ops:
  4.6 3.9 %collective-permute-start = (s32[1,256]{1,0:T(1,128)}, s32[1,256]{1,0:T(1,128)S(1)}, u32[]{:S(2)}, u32[]{:S(2)}) collective-permute-start(s32[1,256]{1,0:T(1,128)} %get-tuple-element.23), channel_id=1, source_target_pairs={{0,32},{32,0},{64,96},{96,64},{128,160},{160,128},{192,224},{224,1... | collective-permute-start | bytes 3080 | tf_op jit(solution)/shard_map/ppermute | solution.py:315
  8.6 6.3 %collective-permute-done = s32[1,256]{1,0:T(1,128)S(1)} collective-permute-done((s32[1,256]{1,0:T(1,128)}, s32[1,256]{1,0:T(1,128)S(1)}, u32[]{:S(2)}, u32[]{:S(2)}) %collective-permute-start) | collective-permute-done | bytes 1056 | tf_op jit(solution)/shard_map/ppermute | solution.py:315
  15.6 4.4 %collective-permute-done.1 = s32[2,256]{1,0:T(2,128)S(1)} collective-permute-done((s32[2,256]{1,0:T(2,128)S(1)}, s32[2,256]{1,0:T(2,128)S(1)}, u32[]{:S(2)}, u32[]{:S(2)}) %collective-permute-start.1) | collective-permute-done | bytes 2080 | tf_op jit(solution)/shard_map/ppermute | solution.py:315
  23.7 4.5 %collective-permute-done.2 = s32[4,256]{1,0:T(4,128)S(1)} collective-permute-done((s32[4,256]{1,0:T(4,128)S(1)}, s32[4,256]{1,0:T(4,128)S(1)}, u32[]{:S(2)}, u32[]{:S(2)}) %collective-permute-start.2) | collective-permute-done | bytes 4128 | tf_op jit(solution)/shard_map/ppermute | solution.py:315
  37.6 5.2 %collective-permute-done.7.refs_2_ = bf16[64,16,128]{2,1,0:T(8,128)(2,1)S(1)} collective-permute-done((bf16[64,16,128]{2,1,0:T(8,128)(2,1)S(1)}, bf16[64,16,128]{2,1,0:T(8,128)(2,1)S(1)}, u32[]{:S(2)}, u32[]{:S(2)}) %collective-permute-start.7) | collective-permute-done | bytes 262176 | tf_op jit(solution)/shard_map/ppermute | solution.py:305
  45.5 6.3 %collective-permute-done.11.refs_4_ = bf16[64,16,128]{2,1,0:T(8,128)(2,1)S(1)} collective-permute-done((bf16[64,16,128]{2,1,0:T(8,128)(2,1)S(1)}, bf16[64,16,128]{2,1,0:T(8,128)(2,1)S(1)}, u32[]{:S(2)}, u32[]{:S(2)}) %collective-permute-start.11) | collective-permute-done | bytes 262176 | tf_op jit(solution)/shard_map/ppermute | solution.py:305
  60.3 6.9 %all-to-all-start = ((bf16[32,17,16,128]{3,2,1,0:T(8,128)(2,1)}), bf16[32,17,16,128]{3,2,1,0:T(8,128)(2,1)}, u32[]{:S(2)}, u32[]{:S(2)}) async-start(bf16[32,17,16,128]{3,2,1,0:T(8,128)(2,1)} %shard_map.101), calls=%async_computation | async-start | bytes 4456448 | tf_op jit(solution)/shard_map/all_to_all | solution.py:400
  70.3 25.7 %all-to-all-done.slabs_ref = bf16[32,17,16,128]{3,2,1,0:T(8,128)(2,1)} async-done(((bf16[32,17,16,128]{3,2,1,0:T(8,128)(2,1)}), bf16[32,17,16,128]{3,2,1,0:T(8,128)(2,1)}, u32[]{:S(2)}, u32[]{:S(2)}) %all-to-all-start) | async-done | bytes 2228256 | tf_op jit(solution)/shard_map/all_to_all | solution.py:400
  96.0 4.9 %all-to-all-start.1 = ((bf16[32,16,16,128]{3,2,1,0:T(8,128)(2,1)}), bf16[32,16,16,128]{3,2,1,0:T(8,128)(2,1)}, u32[]{:S(2)}, u32[]{:S(2)}) async-start(bf16[32,16,16,128]{3,2,1,0:T(8,128)(2,1)} %shard_map.102), calls=%async_computation.1 | async-start | bytes 4194304 | tf_op jit(solution)/shard_map/all_to_all | solution.py:400
  101.9 11.2 %shard_map.104 = bf16[32,16,16,128]{3,2,1,0:T(8,128)(2,1)} custom-call(s32[128]{0:T(128)S(1)} %squeeze.26.tags_ref, bf16[512,1024]{1,0:T(8,128)(2,1)S(1)} %copy-done.6, bf16[1024,1024]{1,0:T(8,128)(2,1)} %constant.123.clone.right_ref, bf16[2,512,512]{2,1,0:T(8,128)(2,1)S(1)} %copy-done.4, bf16[2,512,512]{2,1,0:T(8,128)(2,1)S(1)} %copy-done.5, ...), custom_call_target="tpu_custom_call" | custom-call | flops 4294967296 | bytes 10485760 | tf_op jit(solution)/shard_map/pallas_call | solution.py:406
  113.1 15.5 %all-to-all-done.1.slabs_ref = bf16[32,16,16,128]{3,2,1,0:T(8,128)(2,1)} async-done(((bf16[32,16,16,128]{3,2,1,0:T(8,128)(2,1)}), bf16[32,16,16,128]{3,2,1,0:T(8,128)(2,1)}, u32[]{:S(2)}, u32[]{:S(2)}) %all-to-all-start.1) | async-done | bytes 2097184 | tf_op jit(solution)/shard_map/all_to_all | solution.py:400
  128.6 4.8 %all-to-all-start.3 = ((bf16[32,16,16,128]{3,2,1,0:T(8,128)(2,1)}), bf16[32,16,16,128]{3,2,1,0:T(8,128)(2,1)}, u32[]{:S(2)}, u32[]{:S(2)}) async-start(bf16[32,16,16,128]{3,2,1,0:T(8,128)(2,1)} %shard_map.104), calls=%async_computation.3 | async-start | bytes 4194304 | tf_op jit(solution)/shard_map/all_to_all | solution.py:419
  133.5 11.2 %shard_map.103 = bf16[32,16,16,128]{3,2,1,0:T(8,128)(2,1)} custom-call(s32[128]{0:T(128)S(1)} %squeeze.23.tags_ref, bf16[512,1024]{1,0:T(8,128)(2,1)S(1)} %copy-done.6, bf16[1024,1024]{1,0:T(8,128)(2,1)} %constant.123.clone.right_ref, bf16[2,512,512]{2,1,0:T(8,128)(2,1)S(1)} %copy-done.4, bf16[2,512,512]{2,1,0:T(8,128)(2,1)S(1)} %copy-done.5, ...), custom_call_target="tpu_custom_call" | custom-call | flops 4294967296 | bytes 10485760 | tf_op jit(solution)/shard_map/pallas_call | solution.py:406
  144.6 16.4 %all-to-all-done.3.slots_ref = bf16[32,16,16,128]{3,2,1,0:T(8,128)(2,1)} async-done(((bf16[32,16,16,128]{3,2,1,0:T(8,128)(2,1)}), bf16[32,16,16,128]{3,2,1,0:T(8,128)(2,1)}, u32[]{:S(2)}, u32[]{:S(2)}) %all-to-all-start.3) | async-done | bytes 2097184 | tf_op jit(solution)/shard_map/all_to_all | solution.py:419
  161.0 4.8 %all-to-all-start.2 = ((bf16[32,16,16,128]{3,2,1,0:T(8,128)(2,1)}), bf16[32,16,16,128]{3,2,1,0:T(8,128)(2,1)}, u32[]{:S(2)}, u32[]{:S(2)}) async-start(bf16[32,16,16,128]{3,2,1,0:T(8,128)(2,1)} %shard_map.103), calls=%async_computation.2 | async-start | bytes 4194304 | tf_op jit(solution)/shard_map/all_to_all | solution.py:419
  170.9 22.6 %all-to-all-done.2.slots_ref = bf16[32,16,16,128]{3,2,1,0:T(8,128)(2,1)} async-done(((bf16[32,16,16,128]{3,2,1,0:T(8,128)(2,1)}), bf16[32,16,16,128]{3,2,1,0:T(8,128)(2,1)}, u32[]{:S(2)}, u32[]{:S(2)}) %all-to-all-start.2) | async-done | bytes 2097184 | tf_op jit(solution)/shard_map/all_to_all | solution.py:419
  197.6 3.5 %collective-permute-start.18 = (bf16[32,16,128]{2,1,0:T(8,128)(2,1)S(1)}, bf16[32,16,128]{2,1,0:T(8,128)(2,1)S(1)}, u32[]{:S(2)}, u32[]{:S(2)}) collective-permute-start(bf16[32,16,128]{2,1,0:T(8,128)(2,1)S(1)} %get-tuple-element.50), channel_id=1, source_target_pairs={{0,224},{32,0},{64,32},{96,64},{128,96},{160,128},{192,160},{224,1... | collective-permute-start | bytes 393224 | tf_op jit(solution)/shard_map/ppermute | solution.py:305
  203.7 3.4 %collective-permute-start.19 = (bf16[64,16,128]{2,1,0:T(8,128)(2,1)S(1)}, bf16[64,16,128]{2,1,0:T(8,128)(2,1)S(1)}, u32[]{:S(2)}, u32[]{:S(2)}) collective-permute-start(bf16[64,16,128]{2,1,0:T(8,128)(2,1)S(1)} %pad_maximum_fusion.1), channel_id=1, source_target_pairs={{0,224},{32,0},{64,32},{96,64},{128,96},{160,128},{192,160},{224,1... | collective-permute-start | bytes 786440 | tf_op jit(solution)/shard_map/ppermute | solution.py:305
  207.6 3.7 %collective-permute-done.19 = bf16[64,16,128]{2,1,0:T(8,128)(2,1)S(1)} collective-permute-done((bf16[64,16,128]{2,1,0:T(8,128)(2,1)S(1)}, bf16[64,16,128]{2,1,0:T(8,128)(2,1)S(1)}, u32[]{:S(2)}, u32[]{:S(2)}) %collective-permute-start.19) | collective-permute-done | bytes 262176 | tf_op jit(solution)/shard_map/ppermute | solution.py:305
  211.4 3.4 %collective-permute-start.20 = (bf16[64,16,128]{2,1,0:T(8,128)(2,1)S(1)}, bf16[64,16,128]{2,1,0:T(8,128)(2,1)S(1)}, u32[]{:S(2)}, u32[]{:S(2)}) collective-permute-start(bf16[64,16,128]{2,1,0:T(8,128)(2,1)S(1)} %add_convert_fusion.2), channel_id=1, source_target_pairs={{0,224},{32,0},{64,32},{96,64},{128,96},{160,128},{192,160},{224,1... | collective-permute-start | bytes 786440 | tf_op jit(solution)/shard_map/ppermute | solution.py:305
  215.4 3.3 %collective-permute-done.20 = bf16[64,16,128]{2,1,0:T(8,128)(2,1)S(1)} collective-permute-done((bf16[64,16,128]{2,1,0:T(8,128)(2,1)S(1)}, bf16[64,16,128]{2,1,0:T(8,128)(2,1)S(1)}, u32[]{:S(2)}, u32[]{:S(2)}) %collective-permute-start.20) | collective-permute-done | bytes 262176 | tf_op jit(solution)/shard_map/ppermute | solution.py:305
  218.8 3.8 %collective-permute-start.21 = (bf16[64,16,128]{2,1,0:T(8,128)(2,1)S(1)}, bf16[64,16,128]{2,1,0:T(8,128)(2,1)S(1)}, u32[]{:S(2)}, u32[]{:S(2)}) collective-permute-start(bf16[64,16,128]{2,1,0:T(8,128)(2,1)S(1)} %add_convert_fusion.1), channel_id=1, source_target_pairs={{0,224},{32,0},{64,32},{96,64},{128,96},{160,128},{192,160},{224,1... | collective-permute-start | bytes 786440 | tf_op jit(solution)/shard_map/ppermute | solution.py:305
  226.4 4.5 %collective-permute-done.17 = bf16[64,16,128]{2,1,0:T(8,128)(2,1)S(1)} collective-permute-done((bf16[64,16,128]{2,1,0:T(8,128)(2,1)S(1)}, bf16[64,16,128]{2,1,0:T(8,128)(2,1)S(1)}, u32[]{:S(2)}, u32[]{:S(2)}) %collective-permute-start.17) | collective-permute-done | bytes 262176 | tf_op jit(solution)/shard_map/ppermute | solution.py:305
  233.1 5.0 %collective-permute-start.23 = (bf16[16,16,128]{2,1,0:T(8,128)(2,1)S(1)}, bf16[16,16,128]{2,1,0:T(8,128)(2,1)S(1)}, u32[]{:S(2)}, u32[]{:S(2)}) collective-permute-start(bf16[16,16,128]{2,1,0:T(8,128)(2,1)S(1)} %get-tuple-element.46), channel_id=1, source_target_pairs={{0,2},{1,3},{2,0},{3,1},{4,6},{5,7},{6,4},{7,5},{8,10},{9,11},{10,... | collective-permute-start | bytes 196616 | tf_op jit(solution)/shard_map/ppermute | solution.py:305
  (109 shorter events, 58.3 us)
Async XLA Ops:
  2.6 31.1 %collective-permute-start.6 = (bf16[64,16,128]{2,1,0:T(8,128)(2,1)}, bf16[64,16,128]{2,1,0:T(8,128)(2,1)S(1)}, u32[]{:S(2)}, u32[]{:S(2)}) collective-permute-start(bf16[64,16,128]{2,1,0:T(8,128)(2,1)} %get-tuple-element.24.refs_0_), channel_id=1, source_target_pairs={{0,224},{32,0},{64,32},{96,64},{128,96},{160,128},{192,160},{224,1... | collective-permute-start | bytes 786440 | tf_op jit(solution)/shard_map/ppermute | solution.py:305
  4.4 29.3 %collective-permute-start.9 = (bf16[64,16,128]{2,1,0:T(8,128)(2,1)}, bf16[64,16,128]{2,1,0:T(8,128)(2,1)S(1)}, u32[]{:S(2)}, u32[]{:S(2)}) collective-permute-start(bf16[64,16,128]{2,1,0:T(8,128)(2,1)} %get-tuple-element.24.refs_0_), channel_id=1, source_target_pairs={{0,32},{32,64},{64,96},{96,128},{128,160},{160,192},{192,224},{224... | collective-permute-start | bytes 786440 | tf_op jit(solution)/shard_map/ppermute | solution.py:305
  4.6 10.3 %collective-permute-start = (s32[1,256]{1,0:T(1,128)}, s32[1,256]{1,0:T(1,128)S(1)}, u32[]{:S(2)}, u32[]{:S(2)}) collective-permute-start(s32[1,256]{1,0:T(1,128)} %get-tuple-element.23), channel_id=1, source_target_pairs={{0,32},{32,0},{64,96},{96,64},{128,160},{160,128},{192,224},{224,1... | collective-permute-start | bytes 3080 | tf_op jit(solution)/shard_map/ppermute | solution.py:315
  20.7 7.5 %collective-permute-start.2 = (s32[4,256]{1,0:T(4,128)S(1)}, s32[4,256]{1,0:T(4,128)S(1)}, u32[]{:S(2)}, u32[]{:S(2)}) collective-permute-start(s32[4,256]{1,0:T(4,128)S(1)} %pad_add_fusion.1), channel_id=1, source_target_pairs={{0,128},{32,160},{64,192},{96,224},{128,0},{160,32},{192,64},{224,... | collective-permute-start | bytes 12296 | tf_op jit(solution)/shard_map/ppermute | solution.py:315
  29.2 6.6 %collective-permute-start.5 = (s32[1,256]{1,0:T(1,128)S(1)}, s32[1,256]{1,0:T(1,128)S(1)}, u32[]{:S(2)}, u32[]{:S(2)}) collective-permute-start(s32[1,256]{1,0:T(1,128)S(1)} %reshape.128), channel_id=1, source_target_pairs={{0,3},{1,0},{2,1},{3,2},{4,7},{5,4},{6,5},{7,6},{8,11},{9,8},{10,9... | collective-permute-start | bytes 3080 | tf_op jit(solution)/shard_map/ppermute | solution.py:305
  33.7 9.1 %collective-permute-start.7 = (bf16[64,16,128]{2,1,0:T(8,128)(2,1)S(1)}, bf16[64,16,128]{2,1,0:T(8,128)(2,1)S(1)}, u32[]{:S(2)}, u32[]{:S(2)}) collective-permute-start(bf16[64,16,128]{2,1,0:T(8,128)(2,1)S(1)} %collective-permute-done.6.refs_1_), channel_id=1, source_target_pairs={{0,224},{32,0},{64,32},{96,64},{128,96},{160,128},{192,160},{224,1... | collective-permute-start | bytes 786440 | tf_op jit(solution)/shard_map/ppermute | solution.py:305
  33.7 9.1 %collective-permute-start.10 = (bf16[64,16,128]{2,1,0:T(8,128)(2,1)S(1)}, bf16[64,16,128]{2,1,0:T(8,128)(2,1)S(1)}, u32[]{:S(2)}, u32[]{:S(2)}) collective-permute-start(bf16[64,16,128]{2,1,0:T(8,128)(2,1)S(1)} %collective-permute-done.9.refs_6_), channel_id=1, source_target_pairs={{0,32},{32,64},{64,96},{96,128},{128,160},{160,192},{192,224},{224... | collective-permute-start | bytes 786440 | tf_op jit(solution)/shard_map/ppermute | solution.py:305
  42.8 9.1 %collective-permute-start.8 = (bf16[64,16,128]{2,1,0:T(8,128)(2,1)S(1)}, bf16[64,16,128]{2,1,0:T(8,128)(2,1)S(1)}, u32[]{:S(2)}, u32[]{:S(2)}) collective-permute-start(bf16[64,16,128]{2,1,0:T(8,128)(2,1)S(1)} %collective-permute-done.7.refs_2_), channel_id=1, source_target_pairs={{0,224},{32,0},{64,32},{96,64},{128,96},{160,128},{192,160},{224,1... | collective-permute-start | bytes 786440 | tf_op jit(solution)/shard_map/ppermute | solution.py:305
  42.8 9.0 %collective-permute-start.11 = (bf16[64,16,128]{2,1,0:T(8,128)(2,1)S(1)}, bf16[64,16,128]{2,1,0:T(8,128)(2,1)S(1)}, u32[]{:S(2)}, u32[]{:S(2)}) collective-permute-start(bf16[64,16,128]{2,1,0:T(8,128)(2,1)S(1)} %collective-permute-done.10.refs_5_), channel_id=1, source_target_pairs={{0,32},{32,64},{64,96},{96,128},{128,160},{160,192},{192,224},{224... | collective-permute-start | bytes 786440 | tf_op jit(solution)/shard_map/ppermute | solution.py:305
  51.8 6.0 %collective-permute-start.12 = (bf16[32,16,128]{2,1,0:T(8,128)(2,1)S(1)}, bf16[32,16,128]{2,1,0:T(8,128)(2,1)S(1)}, u32[]{:S(2)}, u32[]{:S(2)}) collective-permute-start(bf16[32,16,128]{2,1,0:T(8,128)(2,1)S(1)} %slice.68), channel_id=1, source_target_pairs={{0,32},{32,64},{64,96},{96,128},{128,160},{160,192},{192,224},{224... | collective-permute-start | bytes 393224 | tf_op jit(solution)/shard_map/ppermute | solution.py:305
  60.3 35.7 %all-to-all-start = ((bf16[32,17,16,128]{3,2,1,0:T(8,128)(2,1)}), bf16[32,17,16,128]{3,2,1,0:T(8,128)(2,1)}, u32[]{:S(2)}, u32[]{:S(2)}) async-start(bf16[32,17,16,128]{3,2,1,0:T(8,128)(2,1)} %shard_map.101), calls=%async_computation | async-start | bytes 4456448 | tf_op jit(solution)/shard_map/all_to_all | solution.py:400
  96.0 32.6 %all-to-all-start.1 = ((bf16[32,16,16,128]{3,2,1,0:T(8,128)(2,1)}), bf16[32,16,16,128]{3,2,1,0:T(8,128)(2,1)}, u32[]{:S(2)}, u32[]{:S(2)}) async-start(bf16[32,16,16,128]{3,2,1,0:T(8,128)(2,1)} %shard_map.102), calls=%async_computation.1 | async-start | bytes 4194304 | tf_op jit(solution)/shard_map/all_to_all | solution.py:400
  128.6 32.5 %all-to-all-start.3 = ((bf16[32,16,16,128]{3,2,1,0:T(8,128)(2,1)}), bf16[32,16,16,128]{3,2,1,0:T(8,128)(2,1)}, u32[]{:S(2)}, u32[]{:S(2)}) async-start(bf16[32,16,16,128]{3,2,1,0:T(8,128)(2,1)} %shard_map.104), calls=%async_computation.3 | async-start | bytes 4194304 | tf_op jit(solution)/shard_map/all_to_all | solution.py:419
  161.0 32.5 %all-to-all-start.2 = ((bf16[32,16,16,128]{3,2,1,0:T(8,128)(2,1)}), bf16[32,16,16,128]{3,2,1,0:T(8,128)(2,1)}, u32[]{:S(2)}, u32[]{:S(2)}) async-start(bf16[32,16,16,128]{3,2,1,0:T(8,128)(2,1)} %shard_map.103), calls=%async_computation.2 | async-start | bytes 4194304 | tf_op jit(solution)/shard_map/all_to_all | solution.py:419
  197.6 6.1 %collective-permute-start.18 = (bf16[32,16,128]{2,1,0:T(8,128)(2,1)S(1)}, bf16[32,16,128]{2,1,0:T(8,128)(2,1)S(1)}, u32[]{:S(2)}, u32[]{:S(2)}) collective-permute-start(bf16[32,16,128]{2,1,0:T(8,128)(2,1)S(1)} %get-tuple-element.50), channel_id=1, source_target_pairs={{0,224},{32,0},{64,32},{96,64},{128,96},{160,128},{192,160},{224,1... | collective-permute-start | bytes 393224 | tf_op jit(solution)/shard_map/ppermute | solution.py:305
  201.1 6.3 %collective-permute-start.14 = (bf16[32,16,128]{2,1,0:T(8,128)(2,1)S(1)}, bf16[32,16,128]{2,1,0:T(8,128)(2,1)S(1)}, u32[]{:S(2)}, u32[]{:S(2)}) collective-permute-start(bf16[32,16,128]{2,1,0:T(8,128)(2,1)S(1)} %get-tuple-element.49), channel_id=1, source_target_pairs={{0,32},{32,64},{64,96},{96,128},{128,160},{160,192},{192,224},{224... | collective-permute-start | bytes 393224 | tf_op jit(solution)/shard_map/ppermute | solution.py:305
  203.7 7.6 %collective-permute-start.19 = (bf16[64,16,128]{2,1,0:T(8,128)(2,1)S(1)}, bf16[64,16,128]{2,1,0:T(8,128)(2,1)S(1)}, u32[]{:S(2)}, u32[]{:S(2)}) collective-permute-start(bf16[64,16,128]{2,1,0:T(8,128)(2,1)S(1)} %pad_maximum_fusion.1), channel_id=1, source_target_pairs={{0,224},{32,0},{64,32},{96,64},{128,96},{160,128},{192,160},{224,1... | collective-permute-start | bytes 786440 | tf_op jit(solution)/shard_map/ppermute | solution.py:305
  207.5 7.7 %collective-permute-start.15 = (bf16[64,16,128]{2,1,0:T(8,128)(2,1)S(1)}, bf16[64,16,128]{2,1,0:T(8,128)(2,1)S(1)}, u32[]{:S(2)}, u32[]{:S(2)}) collective-permute-start(bf16[64,16,128]{2,1,0:T(8,128)(2,1)S(1)} %pad_maximum_fusion), channel_id=1, source_target_pairs={{0,32},{32,64},{64,96},{96,128},{128,160},{160,192},{192,224},{224... | collective-permute-start | bytes 786440 | tf_op jit(solution)/shard_map/ppermute | solution.py:305
  211.4 7.3 %collective-permute-start.20 = (bf16[64,16,128]{2,1,0:T(8,128)(2,1)S(1)}, bf16[64,16,128]{2,1,0:T(8,128)(2,1)S(1)}, u32[]{:S(2)}, u32[]{:S(2)}) collective-permute-start(bf16[64,16,128]{2,1,0:T(8,128)(2,1)S(1)} %add_convert_fusion.2), channel_id=1, source_target_pairs={{0,224},{32,0},{64,32},{96,64},{128,96},{160,128},{192,160},{224,1... | collective-permute-start | bytes 786440 | tf_op jit(solution)/shard_map/ppermute | solution.py:305
  215.3 7.7 %collective-permute-start.16 = (bf16[64,16,128]{2,1,0:T(8,128)(2,1)S(1)}, bf16[64,16,128]{2,1,0:T(8,128)(2,1)S(1)}, u32[]{:S(2)}, u32[]{:S(2)}) collective-permute-start(bf16[64,16,128]{2,1,0:T(8,128)(2,1)S(1)} %add_convert_fusion.4), channel_id=1, source_target_pairs={{0,32},{32,64},{64,96},{96,128},{128,160},{160,192},{192,224},{224... | collective-permute-start | bytes 786440 | tf_op jit(solution)/shard_map/ppermute | solution.py:305
  218.8 7.7 %collective-permute-start.21 = (bf16[64,16,128]{2,1,0:T(8,128)(2,1)S(1)}, bf16[64,16,128]{2,1,0:T(8,128)(2,1)S(1)}, u32[]{:S(2)}, u32[]{:S(2)}) collective-permute-start(bf16[64,16,128]{2,1,0:T(8,128)(2,1)S(1)} %add_convert_fusion.1), channel_id=1, source_target_pairs={{0,224},{32,0},{64,32},{96,64},{128,96},{160,128},{192,160},{224,1... | collective-permute-start | bytes 786440 | tf_op jit(solution)/shard_map/ppermute | solution.py:305
  223.1 7.8 %collective-permute-start.17 = (bf16[64,16,128]{2,1,0:T(8,128)(2,1)S(1)}, bf16[64,16,128]{2,1,0:T(8,128)(2,1)S(1)}, u32[]{:S(2)}, u32[]{:S(2)}) collective-permute-start(bf16[64,16,128]{2,1,0:T(8,128)(2,1)S(1)} %add_convert_fusion.3), channel_id=1, source_target_pairs={{0,32},{32,64},{64,96},{96,128},{128,160},{160,192},{192,224},{224... | collective-permute-start | bytes 786440 | tf_op jit(solution)/shard_map/ppermute | solution.py:305
  231.1 7.9 %collective-permute-start.22 = (bf16[16,16,128]{2,1,0:T(8,128)(2,1)S(1)}, bf16[16,16,128]{2,1,0:T(8,128)(2,1)S(1)}, u32[]{:S(2)}, u32[]{:S(2)}) collective-permute-start(bf16[16,16,128]{2,1,0:T(8,128)(2,1)S(1)} %get-tuple-element.47), channel_id=1, source_target_pairs={{0,1},{1,2},{2,3},{3,0},{4,5},{5,6},{6,7},{7,4},{8,9},{9,10},{10,1... | collective-permute-start | bytes 196616 | tf_op jit(solution)/shard_map/ppermute | solution.py:305
  233.1 8.0 %collective-permute-start.23 = (bf16[16,16,128]{2,1,0:T(8,128)(2,1)S(1)}, bf16[16,16,128]{2,1,0:T(8,128)(2,1)S(1)}, u32[]{:S(2)}, u32[]{:S(2)}) collective-permute-start(bf16[16,16,128]{2,1,0:T(8,128)(2,1)S(1)} %get-tuple-element.46), channel_id=1, source_target_pairs={{0,2},{1,3},{2,0},{3,1},{4,6},{5,7},{6,4},{7,5},{8,10},{9,11},{10,... | collective-permute-start | bytes 196616 | tf_op jit(solution)/shard_map/ppermute | solution.py:305
  (13 other events, 208.1 us)
